TPU v7x, 512 devices: a whole 4x4x16 slice. The times are simulated.
512 devices in a mesh: grp: 4 (over y), row: 128 (over x, z, core).
Axes of the slice: x: 4, y: 4, z: 16, core: 2. Of those that a mesh axis runs over, the one named last changes fastest.
Arguments:
- a_tiles: bfloat16 [1024, 4, 7, 128, 128], P('row', 'grp'), may hold values from -0.5 to 0.5
- a_cols: int32 [1024, 4, 7], P('row', 'grp'), may hold values from 0 to 1023, as said below
- p_tiles: bfloat16 [1024, 4, 128, 128], P('row'), may hold values from -0.5 to 0.5
- p_cols: int32 [1024, 4], replicated, may hold values from 0 to 511, as said below
- c_cols: int32 [512, 16], replicated, may hold values from 0 to 511, as said below
Outputs:
- coarse: float32 [512, 16, 128, 128], P('row', 'grp')
Inputs may be any that keep to these rules, and one draw needn't show every extreme that they name: For fine tile row i in block b = i // 8, every entry of a_cols[i] lies in [max(b - 2, 0) * 8, min(b + 3, 128) * 8). For fine tile row i in block b = i // 8, the entries of p_cols[i] are distinct and lie in [(b - 1) * 4, (b + 2) * 4). For coarse tile row c in block t = c // 4, the entries of c_cols[c] are distinct and lie among the 20 coarse tile rows that start at min(max(t - 2, 0), 123) * 4.
All inputs are finite; a program needn't handle non-finite values.
Results may differ from a plain program's by a relative error of at most 0.0003.
Values may be sent and summed in bfloat16 or wider, within the bound.
A program may use at most 128 MiB of HBM per device.

v0:
```python
import jax
import jax.numpy as jnp
from jax import lax
from jax.sharding import PartitionSpec as P

RATIO = 2


highest = lax.Precision.HIGHEST


def passed_along(x, axis, by):
    size = lax.axis_size(axis)
    pairs = [(i, i + by) for i in range(size) if 0 <= i + by < size]
    return lax.ppermute(x, axis, pairs)


def in_blocks(x, dim, size):
    shape = x.shape
    tiles = x.reshape(*shape[:dim], size, shape[dim] // size, *shape[dim + 1 :])
    return jnp.moveaxis(tiles, dim, 0)


def summed_on_arrival(x, axis, dim):
    tiles = in_blocks(x, dim, lax.axis_size(axis))
    arrived = lax.all_to_all(tiles, axis, split_axis=0, concat_axis=0, tiled=True)
    return arrived.sum(axis=0)


def body(a_tiles, a_cols, p_tiles, p_cols, c_cols):
    fine_rows = a_tiles.shape[0]
    coarse_rows = fine_rows // RATIO
    tile_size = a_tiles.shape[-1]
    position = lax.axis_index("row")
    first_row = position * fine_rows
    fetched_rows = []
    for offset in (2, 1, -1, -2):
        fetched_rows.append(passed_along(p_tiles, "row", offset))
    band_tiles = jnp.concatenate(
        [fetched_rows[0], fetched_rows[1], p_tiles, fetched_rows[2], fetched_rows[3]], axis=0
    )
    padded = jnp.pad(p_cols, ((2 * fine_rows, 2 * fine_rows), (0, 0)), constant_values=-1)
    band_cols = lax.dynamic_slice_in_dim(padded, first_row, 5 * fine_rows, 0)
    own_cols = lax.dynamic_slice_in_dim(p_cols, first_row, fine_rows, 0)
    window = (position - 3) * coarse_rows + jnp.arange(7 * coarse_rows, dtype=jnp.int32)
    base_coarse = (position - 1) * coarse_rows
    local_cols = a_cols[:, 0, :] - (first_row - 2 * fine_rows)

    def fine_row(total, inputs):
        a_row, local_row, own_tiles, own_row_cols = inputs
        fetched = band_tiles[local_row]
        fetched_cols = band_cols[local_row]
        products = jnp.einsum("sxy,spyz->spxz", a_row, fetched, preferred_element_type=jnp.float32)
        placing = (fetched_cols[:, :, None] == window[None, None, :]).astype(jnp.float32)
        spread = jnp.einsum("spxz,spw->wxz", products, placing, precision=highest)
        targets = c_cols[own_row_cols]
        choose = (targets[:, :, None] == window[None, None, :]).astype(jnp.float32)
        chosen = jnp.einsum("qkw,wxz->qkxz", choose, spread, precision=highest)
        row_terms = jnp.einsum(
            "qyx,qkyz->qkxz", own_tiles.astype(jnp.float32), chosen, precision=highest
        )
        local_index = own_row_cols - base_coarse
        return (total.at[local_index].add(row_terms), None)

    initial = jnp.zeros((3 * coarse_rows, c_cols.shape[1], tile_size, tile_size), jnp.float32)
    total = lax.scan(fine_row, initial, (a_tiles[:, 0], local_cols, p_tiles, own_cols))[0]
    center = total[coarse_rows : 2 * coarse_rows]
    for offset, side_block in ((-1, total[:coarse_rows]), (1, total[2 * coarse_rows :])):
        center = center + passed_along(side_block, "row", offset)
    result = summed_on_arrival(center, "grp", 1)
    return result


def solution(mesh):
    return jax.shard_map(
        body,
        mesh=mesh,
        in_specs=(
            P("row", "grp", None, None, None),
            P("row", "grp", None),
            P("row", None, None, None),
            P(),
            P(),
        ),
        out_specs=P("row", "grp", None, None),
        check_vma=False,
    )
```

profile of v0, /device:TPU:6, one launch (start us, length us, event | category | flops | bytes accessed | tf_op | source)
XLA Modules:
  0.0 433.1 jit_solution(5140706142570658629)
XLA Ops:
  5.9 9.2 %collective-permute-start.2 = (bf16[8,4,128,128]{3,2,1,0:T(8,128)(2,1)}, bf16[8,4,128,128]{3,2,1,0:T(8,128)(2,1)}, u32[]{:S(2)}, u32[]{:S(2)}) collective-permute-start(bf16[8,4,128,128]{3,2,1,0:T(8,128)(2,1)} %param.9), channel_id=1, source_target_pairs={{1,0},{2,1},{3,2},{4,3},{5,4},{6,5},{7,6},{8,7},{9,8},{10,9},{11,1... | collective-permute-start | bytes 3145736 | tf_op jit(solution)/shard_map/ppermute | solution.py:15
  22.0 14.1 %collective-permute-done = bf16[8,4,128,128]{3,2,1,0:T(8,128)(2,1)} collective-permute-done((bf16[8,4,128,128]{3,2,1,0:T(8,128)(2,1)}, bf16[8,4,128,128]{3,2,1,0:T(8,128)(2,1)}, u32[]{:S(2)}, u32[]{:S(2)}) %collective-permute-start) | collective-permute-done | bytes 1048608 | tf_op jit(solution)/shard_map/ppermute | solution.py:15
  38.5 8.0 %collective-permute-done.1 = bf16[8,4,128,128]{3,2,1,0:T(8,128)(2,1)} collective-permute-done((bf16[8,4,128,128]{3,2,1,0:T(8,128)(2,1)}, bf16[8,4,128,128]{3,2,1,0:T(8,128)(2,1)}, u32[]{:S(2)}, u32[]{:S(2)}) %collective-permute-start.1) | collective-permute-done | bytes 1048608 | tf_op jit(solution)/shard_map/ppermute | solution.py:15
  53.3 6.1 %broadcast_in_dim.2 = f32[12,16,128,128]{3,2,1,0:T(8,128)} broadcast(f32[]{:T(128)} %constant.23.clone.1), dimensions={} | broadcast | bytes 12582916 | tf_op jit(solution)/shard_map/broadcast_in_dim | solution.py:65
  59.4 258.9 %while.11 = (s32[]{:T(128)}, f32[12,16,128,128]{3,2,1,0:T(8,128)}, s32[8,4]{1,0:T(8,128)S(1)}, s32[]{:T(128)}, s32[512,16]{1,0:T(8,128)S(1)}, /*index=5*/s32[8,7...) while((s32[]{:T(128)}, f32[12,16,128,128]{3,2,1,0:T(8,128)}, ...), condition=%wide.region_2.3_spmd.clone, body=%wide.region_0.2_spmd.clone.sunk | while | flops 2235568640 | bytes 51881796 | solution.py:66
  72.3 5.1 %fusion.57 = f32[4,16,128,128]{2,3,1,0:T(8,128)} fusion(f32[4,16,128,128]{3,1,2,0:T(8,128)S(1)} %fusion.56, bf16[8,4,128,128]{3,2,1,0:T(8,128)(2,1)S(1)} %copy-done.1, s32[]{:T(128)S(6)} %copy.47), kind=kOutput, calls=%fused_computation.7.clone.1 | convolution fusion | flops 1610612736 | bytes 8519684 | tf_op jit(solution)/shard_map/while/body/eval_jaxpr/qyx,qkyz->qkxz/dot_general | solution.py:59
  77.4 5.4 %copy.39 = f32[4,16,128,128]{3,2,1,0:T(8,128)} copy(f32[4,16,128,128]{2,3,1,0:T(8,128)} %fusion.57) | data formatting | bytes 8388608 | tf_op jit(solution)/shard_map/while/body/eval_jaxpr/qyx,qkyz->qkxz/transpose | solution.py:59
  82.8 9.0 %scatter_fusion = f32[12,16,128,128]{3,2,1,0:T(8,128)} fusion(f32[12,16,128,128]{3,2,1,0:T(8,128)} %get-tuple-element.231, s32[4]{0:T(128)S(1)} %get-tuple-element.216, f32[4,16,128,128]{3,2,1,0:T(8,128)} %copy.39), kind=kCustom, calls=%fused_computation.3.clone.clone.1 | custom fusion | flops 1048576 | bytes 12582928 | tf_op jit(solution)/shard_map/while/body/eval_jaxpr/scatter-add | solution.py:63
  104.6 5.1 %fusion.57 = f32[4,16,128,128]{2,3,1,0:T(8,128)} fusion(f32[4,16,128,128]{3,1,2,0:T(8,128)S(1)} %fusion.56, bf16[8,4,128,128]{3,2,1,0:T(8,128)(2,1)S(1)} %copy-done.1, s32[]{:T(128)S(6)} %copy.47), kind=kOutput, calls=%fused_computation.7.clone.1 | convolution fusion | flops 1610612736 | bytes 8519684 | tf_op jit(solution)/shard_map/while/body/eval_jaxpr/qyx,qkyz->qkxz/dot_general | solution.py:59
  109.7 5.4 %copy.39 = f32[4,16,128,128]{3,2,1,0:T(8,128)} copy(f32[4,16,128,128]{2,3,1,0:T(8,128)} %fusion.57) | data formatting | bytes 8388608 | tf_op jit(solution)/shard_map/while/body/eval_jaxpr/qyx,qkyz->qkxz/transpose | solution.py:59
  115.1 9.0 %scatter_fusion = f32[12,16,128,128]{3,2,1,0:T(8,128)} fusion(f32[12,16,128,128]{3,2,1,0:T(8,128)} %get-tuple-element.231, s32[4]{0:T(128)S(1)} %get-tuple-element.216, f32[4,16,128,128]{3,2,1,0:T(8,128)} %copy.39), kind=kCustom, calls=%fused_computation.3.clone.clone.1 | custom fusion | flops 1048576 | bytes 12582928 | tf_op jit(solution)/shard_map/while/body/eval_jaxpr/scatter-add | solution.py:63
  137.0 5.1 %fusion.57 = f32[4,16,128,128]{2,3,1,0:T(8,128)} fusion(f32[4,16,128,128]{3,1,2,0:T(8,128)S(1)} %fusion.56, bf16[8,4,128,128]{3,2,1,0:T(8,128)(2,1)S(1)} %copy-done.1, s32[]{:T(128)S(6)} %copy.47), kind=kOutput, calls=%fused_computation.7.clone.1 | convolution fusion | flops 1610612736 | bytes 8519684 | tf_op jit(solution)/shard_map/while/body/eval_jaxpr/qyx,qkyz->qkxz/dot_general | solution.py:59
  142.1 5.4 %copy.39 = f32[4,16,128,128]{3,2,1,0:T(8,128)} copy(f32[4,16,128,128]{2,3,1,0:T(8,128)} %fusion.57) | data formatting | bytes 8388608 | tf_op jit(solution)/shard_map/while/body/eval_jaxpr/qyx,qkyz->qkxz/transpose | solution.py:59
  147.4 9.0 %scatter_fusion = f32[12,16,128,128]{3,2,1,0:T(8,128)} fusion(f32[12,16,128,128]{3,2,1,0:T(8,128)} %get-tuple-element.231, s32[4]{0:T(128)S(1)} %get-tuple-element.216, f32[4,16,128,128]{3,2,1,0:T(8,128)} %copy.39), kind=kCustom, calls=%fused_computation.3.clone.clone.1 | custom fusion | flops 1048576 | bytes 12582928 | tf_op jit(solution)/shard_map/while/body/eval_jaxpr/scatter-add | solution.py:63
  169.4 5.1 %fusion.57 = f32[4,16,128,128]{2,3,1,0:T(8,128)} fusion(f32[4,16,128,128]{3,1,2,0:T(8,128)S(1)} %fusion.56, bf16[8,4,128,128]{3,2,1,0:T(8,128)(2,1)S(1)} %copy-done.1, s32[]{:T(128)S(6)} %copy.47), kind=kOutput, calls=%fused_computation.7.clone.1 | convolution fusion | flops 1610612736 | bytes 8519684 | tf_op jit(solution)/shard_map/while/body/eval_jaxpr/qyx,qkyz->qkxz/dot_general | solution.py:59
  174.4 5.4 %copy.39 = f32[4,16,128,128]{3,2,1,0:T(8,128)} copy(f32[4,16,128,128]{2,3,1,0:T(8,128)} %fusion.57) | data formatting | bytes 8388608 | tf_op jit(solution)/shard_map/while/body/eval_jaxpr/qyx,qkyz->qkxz/transpose | solution.py:59
  179.8 9.0 %scatter_fusion = f32[12,16,128,128]{3,2,1,0:T(8,128)} fusion(f32[12,16,128,128]{3,2,1,0:T(8,128)} %get-tuple-element.231, s32[4]{0:T(128)S(1)} %get-tuple-element.216, f32[4,16,128,128]{3,2,1,0:T(8,128)} %copy.39), kind=kCustom, calls=%fused_computation.3.clone.clone.1 | custom fusion | flops 1048576 | bytes 12582928 | tf_op jit(solution)/shard_map/while/body/eval_jaxpr/scatter-add | solution.py:63
  201.7 5.1 %fusion.57 = f32[4,16,128,128]{2,3,1,0:T(8,128)} fusion(f32[4,16,128,128]{3,1,2,0:T(8,128)S(1)} %fusion.56, bf16[8,4,128,128]{3,2,1,0:T(8,128)(2,1)S(1)} %copy-done.1, s32[]{:T(128)S(6)} %copy.47), kind=kOutput, calls=%fused_computation.7.clone.1 | convolution fusion | flops 1610612736 | bytes 8519684 | tf_op jit(solution)/shard_map/while/body/eval_jaxpr/qyx,qkyz->qkxz/dot_general | solution.py:59
  206.8 5.4 %copy.39 = f32[4,16,128,128]{3,2,1,0:T(8,128)} copy(f32[4,16,128,128]{2,3,1,0:T(8,128)} %fusion.57) | data formatting | bytes 8388608 | tf_op jit(solution)/shard_map/while/body/eval_jaxpr/qyx,qkyz->qkxz/transpose | solution.py:59
  212.2 9.0 %scatter_fusion = f32[12,16,128,128]{3,2,1,0:T(8,128)} fusion(f32[12,16,128,128]{3,2,1,0:T(8,128)} %get-tuple-element.231, s32[4]{0:T(128)S(1)} %get-tuple-element.216, f32[4,16,128,128]{3,2,1,0:T(8,128)} %copy.39), kind=kCustom, calls=%fused_computation.3.clone.clone.1 | custom fusion | flops 1048576 | bytes 12582928 | tf_op jit(solution)/shard_map/while/body/eval_jaxpr/scatter-add | solution.py:63
  234.1 5.1 %fusion.57 = f32[4,16,128,128]{2,3,1,0:T(8,128)} fusion(f32[4,16,128,128]{3,1,2,0:T(8,128)S(1)} %fusion.56, bf16[8,4,128,128]{3,2,1,0:T(8,128)(2,1)S(1)} %copy-done.1, s32[]{:T(128)S(6)} %copy.47), kind=kOutput, calls=%fused_computation.7.clone.1 | convolution fusion | flops 1610612736 | bytes 8519684 | tf_op jit(solution)/shard_map/while/body/eval_jaxpr/qyx,qkyz->qkxz/dot_general | solution.py:59
  239.2 5.4 %copy.39 = f32[4,16,128,128]{3,2,1,0:T(8,128)} copy(f32[4,16,128,128]{2,3,1,0:T(8,128)} %fusion.57) | data formatting | bytes 8388608 | tf_op jit(solution)/shard_map/while/body/eval_jaxpr/qyx,qkyz->qkxz/transpose | solution.py:59
  244.6 9.0 %scatter_fusion = f32[12,16,128,128]{3,2,1,0:T(8,128)} fusion(f32[12,16,128,128]{3,2,1,0:T(8,128)} %get-tuple-element.231, s32[4]{0:T(128)S(1)} %get-tuple-element.216, f32[4,16,128,128]{3,2,1,0:T(8,128)} %copy.39), kind=kCustom, calls=%fused_computation.3.clone.clone.1 | custom fusion | flops 1048576 | bytes 12582928 | tf_op jit(solution)/shard_map/while/body/eval_jaxpr/scatter-add | solution.py:63
  266.4 5.1 %fusion.57 = f32[4,16,128,128]{2,3,1,0:T(8,128)} fusion(f32[4,16,128,128]{3,1,2,0:T(8,128)S(1)} %fusion.56, bf16[8,4,128,128]{3,2,1,0:T(8,128)(2,1)S(1)} %copy-done.1, s32[]{:T(128)S(6)} %copy.47), kind=kOutput, calls=%fused_computation.7.clone.1 | convolution fusion | flops 1610612736 | bytes 8519684 | tf_op jit(solution)/shard_map/while/body/eval_jaxpr/qyx,qkyz->qkxz/dot_general | solution.py:59
  271.5 5.4 %copy.39 = f32[4,16,128,128]{3,2,1,0:T(8,128)} copy(f32[4,16,128,128]{2,3,1,0:T(8,128)} %fusion.57) | data formatting | bytes 8388608 | tf_op jit(solution)/shard_map/while/body/eval_jaxpr/qyx,qkyz->qkxz/transpose | solution.py:59
  276.9 9.0 %scatter_fusion = f32[12,16,128,128]{3,2,1,0:T(8,128)} fusion(f32[12,16,128,128]{3,2,1,0:T(8,128)} %get-tuple-element.231, s32[4]{0:T(128)S(1)} %get-tuple-element.216, f32[4,16,128,128]{3,2,1,0:T(8,128)} %copy.39), kind=kCustom, calls=%fused_computation.3.clone.clone.1 | custom fusion | flops 1048576 | bytes 12582928 | tf_op jit(solution)/shard_map/while/body/eval_jaxpr/scatter-add | solution.py:63
  298.8 5.1 %fusion.57 = f32[4,16,128,128]{2,3,1,0:T(8,128)} fusion(f32[4,16,128,128]{3,1,2,0:T(8,128)S(1)} %fusion.56, bf16[8,4,128,128]{3,2,1,0:T(8,128)(2,1)S(1)} %copy-done.1, s32[]{:T(128)S(6)} %copy.47), kind=kOutput, calls=%fused_computation.7.clone.1 | convolution fusion | flops 1610612736 | bytes 8519684 | tf_op jit(solution)/shard_map/while/body/eval_jaxpr/qyx,qkyz->qkxz/dot_general | solution.py:59
  303.9 5.4 %copy.39 = f32[4,16,128,128]{3,2,1,0:T(8,128)} copy(f32[4,16,128,128]{2,3,1,0:T(8,128)} %fusion.57) | data formatting | bytes 8388608 | tf_op jit(solution)/shard_map/while/body/eval_jaxpr/qyx,qkyz->qkxz/transpose | solution.py:59
  309.3 9.0 %scatter_fusion = f32[12,16,128,128]{3,2,1,0:T(8,128)} fusion(f32[12,16,128,128]{3,2,1,0:T(8,128)} %get-tuple-element.231, s32[4]{0:T(128)S(1)} %get-tuple-element.216, f32[4,16,128,128]{3,2,1,0:T(8,128)} %copy.39), kind=kCustom, calls=%fused_computation.3.clone.clone.1 | custom fusion | flops 1048576 | bytes 12582928 | tf_op jit(solution)/shard_map/while/body/eval_jaxpr/scatter-add | solution.py:63
  326.7 43.6 %collective-permute-done.4 = f32[4,16,128,128]{3,2,1,0:T(8,128)S(1)} collective-permute-done((f32[4,16,128,128]{3,2,1,0:T(8,128)S(1)}, f32[4,16,128,128]{3,2,1,0:T(8,128)S(1)}, u32[]{:S(2)}, u32[]{:S(2)}) %collective-permute-start.4) | collective-permute-done | bytes 4194336 | tf_op jit(solution)/shard_map/ppermute | solution.py:15
  370.3 5.9 %collective-permute-done.5 = f32[4,16,128,128]{3,2,1,0:T(8,128)S(1)} collective-permute-done((f32[4,16,128,128]{3,2,1,0:T(8,128)S(1)}, f32[4,16,128,128]{3,2,1,0:T(8,128)S(1)}, u32[]{:S(2)}, u32[]{:S(2)}) %collective-permute-start.5) | collective-permute-done | bytes 4194336 | tf_op jit(solution)/shard_map/ppermute | solution.py:15
  380.3 49.3 %all_to_all.5 = f32[4,4,4,128,128]{4,3,2,1,0:T(8,128)} all-to-all(f32[4,4,4,128,128]{4,3,2,1,0:T(8,128)S(1)} %copy.24), channel_id=1, replica_groups=mesh['grp'=4,'row'=128] {'grp'}, dimensions={0} | all-to-all | bytes 8388608 | tf_op jit(solution)/shard_map/all_to_all | solution.py:26
  (136 shorter events, 140.6 us)
Async XLA Ops:
  0.0 48.8 %copy-start = (bf16[8,4,128,128]{3,2,1,0:T(8,128)(2,1)S(1)}, bf16[8,4,128,128]{3,2,1,0:T(8,128)(2,1)}, u32[]{:S(2)}) copy-start(bf16[8,4,128,128]{3,2,1,0:T(8,128)(2,1)} %param.9) | copy-start | bytes 3145732
  0.0 36.1 %collective-permute-start = (bf16[8,4,128,128]{3,2,1,0:T(8,128)(2,1)}, bf16[8,4,128,128]{3,2,1,0:T(8,128)(2,1)}, u32[]{:S(2)}, u32[]{:S(2)}) collective-permute-start(bf16[8,4,128,128]{3,2,1,0:T(8,128)(2,1)} %param.9), channel_id=1, source_target_pairs={{0,2},{1,3},{2,4},{3,5},{4,6},{5,7},{6,8},{7,9},{8,10},{9,11},{10,... | collective-permute-start | bytes 3145736 | tf_op jit(solution)/shard_map/ppermute | solution.py:15
  4.0 42.5 %collective-permute-start.1 = (bf16[8,4,128,128]{3,2,1,0:T(8,128)(2,1)}, bf16[8,4,128,128]{3,2,1,0:T(8,128)(2,1)}, u32[]{:S(2)}, u32[]{:S(2)}) collective-permute-start(bf16[8,4,128,128]{3,2,1,0:T(8,128)(2,1)} %param.9), channel_id=1, source_target_pairs={{0,1},{1,2},{2,3},{3,4},{4,5},{5,6},{6,7},{7,8},{8,9},{9,10},{10,1... | collective-permute-start | bytes 3145736 | tf_op jit(solution)/shard_map/ppermute | solution.py:15
  5.9 44.0 %collective-permute-start.2 = (bf16[8,4,128,128]{3,2,1,0:T(8,128)(2,1)}, bf16[8,4,128,128]{3,2,1,0:T(8,128)(2,1)}, u32[]{:S(2)}, u32[]{:S(2)}) collective-permute-start(bf16[8,4,128,128]{3,2,1,0:T(8,128)(2,1)} %param.9), channel_id=1, source_target_pairs={{1,0},{2,1},{3,2},{4,3},{5,4},{6,5},{7,6},{8,7},{9,8},{10,9},{11,1... | collective-permute-start | bytes 3145736 | tf_op jit(solution)/shard_map/ppermute | solution.py:15
  15.1 37.1 %collective-permute-start.3 = (bf16[8,4,128,128]{3,2,1,0:T(8,128)(2,1)}, bf16[8,4,128,128]{3,2,1,0:T(8,128)(2,1)S(1)}, u32[]{:S(2)}, u32[]{:S(2)}) collective-permute-start(bf16[8,4,128,128]{3,2,1,0:T(8,128)(2,1)} %param.9), channel_id=1, source_target_pairs={{2,0},{3,1},{4,2},{5,3},{6,4},{7,5},{8,6},{9,7},{10,8},{11,9},{12,... | collective-permute-start | bytes 3145736 | tf_op jit(solution)/shard_map/ppermute | solution.py:15
  70.4 1.9 copy-start.1
  102.8 1.9 copy-start.1
  135.1 1.9 copy-start.1
  167.5 1.9 copy-start.1
  199.8 1.9 copy-start.1
  232.2 1.9 copy-start.1
  264.5 1.9 copy-start.1
  296.9 1.9 copy-start.1
  322.3 47.9 %collective-permute-start.4 = (f32[4,16,128,128]{3,2,1,0:T(8,128)S(1)}, f32[4,16,128,128]{3,2,1,0:T(8,128)S(1)}, u32[]{:S(2)}, u32[]{:S(2)}) collective-permute-start(f32[4,16,128,128]{3,2,1,0:T(8,128)S(1)} %get-tuple-element.145), channel_id=1, source_target_pairs={{1,0},{2,1},{3,2},{4,3},{5,4},{6,5},{7,6},{8,7},{9,8},{10,9},{11,1... | collective-permute-start | bytes 12582920 | tf_op jit(solution)/shard_map/ppermute | solution.py:15
  324.3 51.9 %collective-permute-start.5 = (f32[4,16,128,128]{3,2,1,0:T(8,128)S(1)}, f32[4,16,128,128]{3,2,1,0:T(8,128)S(1)}, u32[]{:S(2)}, u32[]{:S(2)}) collective-permute-start(f32[4,16,128,128]{3,2,1,0:T(8,128)S(1)} %get-tuple-element.146), channel_id=1, source_target_pairs={{0,1},{1,2},{2,3},{3,4},{4,5},{5,6},{6,7},{7,8},{8,9},{9,10},{10,1... | collective-permute-start | bytes 12582920 | tf_op jit(solution)/shard_map/ppermute | solution.py:15
where the time goes:
time: 435 us; the launch traced here: 433 us
  local copies, waits for them, and re-layouts  116 us (27%)
  matrix products  92.8 us (21%)
  other arithmetic  79.5 us (18%)
  waiting for transfers between devices  71.7 us (16%)
  blocking collectives  49.3 us (11%)
  starting transfers between devices  23.6 us (5%)
    scatter-add x8, other arithmetic, fine_row(): return (total.at[local_index].add(row_terms), None)  72 us
    ppermute x6, waiting for transfers between devices, passed_along(): return lax.ppermute(x, axis, pairs)  71.7 us
    all_to_all x1, blocking collectives, summed_on_arrival(): lax.all_to_all(tiles, axis, split_axis=0, concat_axis=0, tiled=True)  49.3 us
    transpose x8, local copies, waits for them, and re-layouts, fine_row(): jnp.einsum('qyx,qkyz->qkxz', own_tiles.astype(jnp.float32), chosen, preci...  42.9 us
    dot_general x8, matrix products, fine_row(): jnp.einsum('qyx,qkyz->qkxz', own_tiles.astype(jnp.float32), chosen, preci...  40.7 us
    dot_general x8, matrix products, fine_row(): spread = jnp.einsum('spxz,spw->wxz', products, placing, precision=highest)  25.8 us
    gather x8, local copies, waits for them, and re-layouts, fine_row(): fetched = band_tiles[local_row]  25.7 us
    ppermute x6, starting transfers between devices, passed_along(): return lax.ppermute(x, axis, pairs)  23.6 us
  transfers between devices with their start and end apart: 6, of which 4 were waited for; matrix products, arithmetic and copies ran while one was open for 2% of the time, Pallas kernels for 0%

commit v1 on v0

v1 whole, which is shorter than its diff:
```python
import jax
import jax.numpy as jnp
from jax import lax
from jax.experimental import pallas as pl
from jax.experimental.pallas import tpu as pltpu
from jax.sharding import PartitionSpec as P

MESH = pl.DeviceIdType.MESH
F32 = jnp.float32
BF16 = jnp.bfloat16
STEPS = (2, 1, 3, 0)


def index_table(a_cols, p_cols, c_cols):
    rows, cols = 8, 4
    position = lax.axis_index("row")
    first = position * rows
    base = (position - 3) * cols
    padded = jnp.pad(p_cols, ((2 * rows, 2 * rows), (0, 0)), constant_values=-1000)
    band = lax.dynamic_slice_in_dim(padded, first, 5 * rows, 0) - base
    tile = jnp.arange(4, dtype=jnp.int32)
    window = jnp.arange(28, dtype=jnp.int32)
    place = jnp.where(band[:, :, None] == window, tile[None, :, None], 4).min(axis=1)
    own = lax.dynamic_slice_in_dim(p_cols, first, rows, 0) - (position - 1) * cols
    coarse = jnp.arange(12, dtype=jnp.int32)
    which = jnp.where(own[:, :, None] == coarse, tile[None, :, None], 4).min(axis=1).T
    padded_c = jnp.pad(c_cols, ((cols, cols), (0, 0)))
    target = lax.dynamic_slice_in_dim(padded_c, position * cols, 12, 0) - base
    target = jnp.where((target >= 0) & (target < 28), target, 28)
    local = a_cols[:, 0, :] - (first - 2 * rows)

    def wide(x):
        return jnp.pad(x, ((0, 0), (0, 128 - x.shape[1])))

    return jnp.concatenate([wide(place), wide(local), wide(target), wide(which)], axis=0), wide(local)


def kernel(
    tab, cols_hbm, a_hbm, p_hbm, out_hbm,
    a_own, a_far, p_own, p_turn, band, spreadable, placed, window, lower, upper,
    from_next, from_prev, center, gathered, out_v, cols_v, cols_s,
    load_sem, a_send, a_recv, c_send, c_recv, p_send, p_recv, s_send, s_recv, g_send, g_recv, out_sem,
):
    grp = lax.axis_index("grp")
    row = lax.axis_index("row")
    n_row = lax.axis_size("row")
    core = lax.rem(row, 2)
    half = lax.rem(grp, 2)

    def along_row(by):
        return (grp, lax.rem(row + by + n_row, n_row))

    def along_grp(by):
        return (lax.rem(grp + by, 4), row)

    partner = (jnp.where(core == 0, grp + 1 - 2 * half, 3 - grp), row)
    sibling = (grp, row + 1 - 2 * core)

    load_p = pltpu.make_async_copy(p_hbm, p_own, load_sem.at[0])
    load_p.start()
    load_a = pltpu.make_async_copy(a_hbm, a_own, load_sem.at[1])
    load_a.start()

    barrier = pltpu.get_barrier_semaphore()
    peers = [along_grp(1), along_grp(2), along_grp(3)] + [along_row(by) for by in (1, -1, 2, -2)]
    for peer in peers:
        pl.semaphore_signal(barrier, inc=1, device_id=peer, device_id_type=MESH)
    pl.semaphore_wait(barrier, len(peers))

    def remote(src, dst, send, recv, device):
        return pltpu.make_async_remote_copy(
            src_ref=src, dst_ref=dst, send_sem=send, recv_sem=recv, device_id=device, device_id_type=MESH
        )

    def a_copy(i):
        return remote(a_hbm.at[i], a_far.at[i], a_send.at[i], a_recv.at[i], partner)

    cols_copy = remote(cols_hbm, cols_v, c_send, c_recv, partner)
    cols_copy.start()
    for i in range(8):
        a_copy(i).start()

    left = lax.broadcasted_iota(jnp.int32, (128, 128), 1) < 64

    def turn(x):
        return pltpu.roll(x.astype(F32), 64, 1).astype(x.dtype)

    load_p.wait()

    def halve(i, carry):
        for pair in range(2):
            x, y = p_own[i, 2 * pair], p_own[i, 2 * pair + 1]
            x_turned, y_turned = turn(x), turn(y)
            first = jnp.where(left, x, y_turned)
            second = jnp.where(left, x_turned, y)
            band[2, i, pair] = jnp.where(half == 0, first, second)
        return carry

    lax.fori_loop(0, 8, halve, 0)

    def transpose(i, carry):
        for q in range(4):
            p_turn[i, q] = p_own[i, q].T
        p_turn[i, 4] = jnp.zeros((128, 128), BF16)
        return carry

    lax.fori_loop(0, 8, transpose, 0)

    up_slot = 3 - 2 * core
    there = 1 + 2 * core
    forward_slot = 4 - 4 * core
    p_next = remote(band.at[2], band.at[0], p_send.at[0], p_recv.at[0], along_row(2))
    p_prev = remote(band.at[2], band.at[4], p_send.at[1], p_recv.at[4], along_row(-2))
    p_sib = remote(band.at[2], band.at[there], p_send.at[2], p_recv.at[there], sibling)
    p_fwd = remote(band.at[forward_slot], band.at[up_slot], p_send.at[3], p_recv.at[up_slot], sibling)
    p_next.start()
    p_prev.start()
    p_sib.start()

    spreadable[4] = jnp.zeros((128, 128), BF16)

    def place_block(slot):
        def place(n, carry):
            line = slot * 8 + n
            for pair in range(2):
                x = band[slot, n, pair]
                turned = turn(x)
                spreadable[2 * pair] = jnp.where(left, x, turned)
                spreadable[2 * pair + 1] = jnp.where(left, turned, x)
            for w in range(14):
                first = spreadable[tab[line, 2 * w]]
                second = spreadable[tab[line, 2 * w + 1]]
                placed[line, w // 2, :, (w % 2) * 128 : (w % 2 + 1) * 128] = jnp.where(left, first, second)
            return carry

        lax.fori_loop(0, 8, place, 0)

    def arrived(slot):
        remote(band.at[slot], band.at[slot], p_send.at[0], p_recv.at[slot], sibling).wait_recv()

    place_block(2)
    arrived(up_slot)
    place_block(up_slot)
    arrived(forward_slot)
    p_fwd.start()
    place_block(forward_slot)
    arrived(4 - forward_slot)
    place_block(4 - forward_slot)
    arrived(4 - up_slot)
    place_block(4 - up_slot)

    cols_copy.wait_recv()
    to_smem = pltpu.make_async_copy(cols_v, cols_s, load_sem.at[2])
    to_smem.start()
    to_smem.wait()
    load_a.wait()

    def fine_row(i, carry):
        window[i, 28] = jnp.zeros((128, 128), BF16)
        a_copy(i).wait_recv()
        lhs = jnp.concatenate([a_own[i, s] for s in range(7)] + [a_far[i, s] for s in range(7)], axis=1)
        lines = [tab[40 + i, s] for s in range(7)] + [cols_s[i, s] for s in range(7)]
        for n in range(7):
            rhs = jnp.concatenate([placed[line, n] for line in lines], axis=0)
            acc = jnp.dot(lhs, rhs, preferred_element_type=F32)
            for u in range(2):
                value = acc[:, u * 128 : (u + 1) * 128]
                high = value.astype(BF16).astype(F32)
                low = value - high
                window[i, 4 * n + 2 * u] = jnp.where(left, high, pltpu.roll(low, 64, 1)).astype(BF16)
                window[i, 4 * n + 2 * u + 1] = jnp.where(left, pltpu.roll(high, 64, 1), low).astype(BF16)
        return carry

    lax.fori_loop(0, 8, fine_row, 0)

    def quarter(t):
        step = jnp.where(t == 0, STEPS[0], jnp.where(t == 1, STEPS[1], jnp.where(t == 2, STEPS[2], STEPS[3])))
        return lax.rem(grp + step, 4)

    def coarse_tiles(c, t):
        lhs = jnp.concatenate([p_turn[i, tab[60 + c, i]] for i in range(8)], axis=1)
        k = quarter(t) * 4
        tiles = []
        for pair in range(2):
            first = tab[48 + c, k + 2 * pair]
            second = tab[48 + c, k + 2 * pair + 1]
            rhs = jnp.concatenate(
                [jnp.concatenate([window[i, first], window[i, second]], axis=1) for i in range(8)], axis=0
            )
            acc = jnp.dot(lhs, rhs, preferred_element_type=F32)
            x, y = acc[:, :128], acc[:, 128:]
            tiles.append(jnp.where(left, x, y) + pltpu.roll(jnp.where(left, y, x), 64, 1))
        return tiles

    def lower_copy(c, t):
        return remote(lower.at[c, t], from_next.at[c, t], s_send.at[0, c, t], s_recv.at[0, c, t], along_row(-1))

    def upper_copy(c, t):
        return remote(upper.at[c, t], from_prev.at[c, t], s_send.at[1, c, t], s_recv.at[1, c, t], along_row(1))

    def sides(c):
        def one(t, carry):
            for pair, tile in enumerate(coarse_tiles(c, t)):
                lower[c, t, pair] = tile
            for pair, tile in enumerate(coarse_tiles(8 + c, t)):
                upper[c, t, pair] = tile

            @pl.when(t > 0)
            def _():
                lower_copy(c, t - 1).start()
                upper_copy(c, t - 1).start()

            return carry

        lax.fori_loop(0, 4, one, 0)
        lower_copy(c, 3).start()
        upper_copy(c, 3).start()

    def middle(c):
        def one(t, carry):
            for pair, tile in enumerate(coarse_tiles(4 + c, t)):
                center[c, t, pair] = tile
            return carry

        lax.fori_loop(0, 4, one, 0)

    def group_copy(c, t):
        return remote(
            center.at[c, t], gathered.at[t, c], g_send.at[t, c], g_recv.at[t, c], along_grp(STEPS[t])
        )

    def absorb(c):
        for t in range(4):
            lower_copy(c, t).wait_recv()
            upper_copy(c, t).wait_recv()
            center[c, t] = center[c, t] + (from_next[c, t] + from_prev[c, t])
            if t > 0:
                group_copy(c, t - 1).start()

    def out_copy(c):
        return pltpu.make_async_copy(out_v.at[c], out_hbm.at[c], out_sem.at[c])

    def finish(c):
        for t in range(3):
            group_copy(c, t).wait_recv()
        for pair in range(2):
            same = center[c, 3, pair] + gathered[0, c, pair]
            other = gathered[1, c, pair] + gathered[2, c, pair]
            x = jnp.where(half == 0, same, other)
            y = jnp.where(half == 0, other, same)
            out_v[c, 2 * pair] = jnp.where(left, x, pltpu.roll(y, 64, 1))
            out_v[c, 2 * pair + 1] = jnp.where(left, pltpu.roll(x, 64, 1), y)
        out_copy(c).start()

    sides(0)
    middle(0)
    sides(1)
    absorb(0)
    middle(1)
    sides(2)
    absorb(1)
    middle(2)
    sides(3)
    absorb(2)
    middle(3)
    absorb(3)
    for c in range(4):
        finish(c)

    cols_copy.wait_send()
    for i in range(8):
        a_copy(i).wait_send()
    p_next.wait_send()
    p_prev.wait_send()
    p_sib.wait_send()
    p_fwd.wait_send()
    for c in range(4):
        for t in range(4):
            lower_copy(c, t).wait_send()
            upper_copy(c, t).wait_send()
        for t in range(3):
            group_copy(c, t).wait_send()
        out_copy(c).wait()


def body(a_tiles, a_cols, p_tiles, p_cols, c_cols):
    table, local = index_table(a_cols, p_cols, c_cols)
    dma = pltpu.SemaphoreType.DMA
    anywhere = pl.BlockSpec(memory_space=pl.ANY)
    return pl.pallas_call(
        kernel,
        out_shape=jax.ShapeDtypeStruct((4, 4, 128, 128), F32),
        in_specs=[pl.BlockSpec(memory_space=pltpu.SMEM), anywhere, anywhere, anywhere],
        out_specs=anywhere,
        scratch_shapes=[
            pltpu.VMEM((8, 7, 128, 128), BF16),
            pltpu.VMEM((8, 7, 128, 128), BF16),
            pltpu.VMEM((8, 4, 128, 128), BF16),
            pltpu.VMEM((8, 5, 128, 128), BF16),
            pltpu.VMEM((5, 8, 2, 128, 128), BF16),
            pltpu.VMEM((5, 128, 128), BF16),
            pltpu.VMEM((40, 7, 128, 256), BF16),
            pltpu.VMEM((8, 29, 128, 128), BF16),
            pltpu.VMEM((4, 4, 2, 128, 128), F32),
            pltpu.VMEM((4, 4, 2, 128, 128), F32),
            pltpu.VMEM((4, 4, 2, 128, 128), F32),
            pltpu.VMEM((4, 4, 2, 128, 128), F32),
            pltpu.VMEM((4, 4, 2, 128, 128), F32),
            pltpu.VMEM((3, 4, 2, 128, 128), F32),
            pltpu.VMEM((4, 4, 128, 128), F32),
            pltpu.VMEM((8, 128), jnp.int32),
            pltpu.SMEM((8, 128), jnp.int32),
            dma((3,)),
            dma((8,)),
            dma((8,)),
            dma,
            dma,
            dma((4,)),
            dma((5,)),
            dma((2, 4, 4)),
            dma((2, 4, 4)),
            dma((3, 4)),
            dma((3, 4)),
            dma((4,)),
        ],
        compiler_params=pltpu.CompilerParams(
            collective_id=0, has_side_effects=True, vmem_limit_bytes=60 * 1024 * 1024
        ),
        cost_estimate=pl.CostEstimate(flops=4_000_000_000, bytes_accessed=8_000_000, transcendentals=0),
    )(table, local, a_tiles.reshape(8, 7, 128, 128), p_tiles)


def solution(mesh):
    return jax.shard_map(
        body,
        mesh=mesh,
        in_specs=(
            P("row", "grp", None, None, None),
            P("row", "grp", None),
            P("row", None, None, None),
            P(),
            P(),
        ),
        out_specs=P("row", "grp", None, None),
        check_vma=False,
    )
```

time: 435 us -> 84.7 us (0.19)
  the two profiles are of different devices: /device:TPU:6 before, /device:TPU:1 now
where the time goes in v1:
time: 84.7 us; the launch traced here: 84.3 us
  Pallas kernels  77.8 us (92%)
  local copies, waits for them, and re-layouts  4.12 us (5%)
  other arithmetic  2.31 us (3%)
    pallas_call x1, Pallas kernels, body(): pl.pallas_call(kernel, out_shape=jax.ShapeDtypeStruct((4, 4, 128, 128), F...  77.8 us
    unnamed x5, local copies, waits for them, and re-layouts  3.94 us

profile of v1, /device:TPU:1, one launch (start us, length us, event | category | flops | bytes accessed | tf_op | source)
XLA Modules:
  0.0 84.3 jit_solution(13465451849917540495)
XLA Ops:
  0.0 0.8 dynamic-slice_subtract_fusion
  0.8 0.8 fusion.1
  1.5 0.1 select_reduce_fusion.1
  1.6 0.1 copy.13
  1.7 0.8 copy.11
  2.5 0.0 copy-start
  2.5 0.1 select_reduce_fusion
  2.5 0.1 copy.10
  2.6 0.9 %copy.12 = s32[512,16]{1,0:T(8,128)S(1)} copy(s32[512,16]{0,1:T(8,128)} %param.9) | data formatting | bytes 65536 | tf_op args[4]
  3.5 0.6 pad_add_fusion.tab
  4.2 0.0 copy-done
  4.2 77.8 %shard_map.55 = f32[4,4,128,128]{3,2,1,0:T(8,128)} custom-call(s32[72,128]{1,0:T(8,128)} %pad_add_fusion.tab, s32[8,128]{1,0:T(8,128)} %copy-done, bf16[8,7,128,128]{3,2,1,0:T(8,128)(2,1)} %bitcast.5, bf16[8,4,128,128]{3,2,1,0:T(8,128)(2,1)} %p_hbm.1), custom_call_target="tpu_custom_call" | custom-call | flops 4000000000 | bytes 8000000 | tf_op jit(solution)/shard_map/pallas_call | solution.py:290
  82.0 2.3 %copy.15 = f32[4,4,128,128]{3,2,1,0:T(8,128)} copy(f32[4,4,128,128]{3,2,1,0:T(8,128)} %shard_map.55) | data formatting | bytes 2097152
  (3 shorter events, 0.0 us)
Async XLA Ops:
  2.5 1.7 %copy-start = (s32[8,128]{1,0:T(8,128)}, s32[8,128]{1,0:T(8,128)S(1)}, u32[]{:S(2)}) copy-start(s32[8,128]{1,0:T(8,128)S(1)} %pad.27.cols_hbm) | copy-start | bytes 12292

commit v2 on v1

v2 whole, which is shorter than its diff:
```python
import jax
import jax.numpy as jnp
from jax import lax
from jax.experimental import pallas as pl
from jax.experimental.pallas import tpu as pltpu
from jax.sharding import PartitionSpec as P

MESH = pl.DeviceIdType.MESH
F32 = jnp.float32
BF16 = jnp.bfloat16
I32 = jnp.int32
PLACE, WHICH, TARGET = 0, 32, 48
BEHIND = 4


def kernel(
    a_cols_hbm, p_cols_hbm, c_cols_hbm, a_hbm, p_hbm, out_v,
    a_own, a_far, p_own, p_turn, band, spreadable, placed, window, outer, inner,
    from_outer, from_inner, center, gathered, p_cols_v, c_cols_v, far_cols_v, tab_v, tab, own_cols, far_cols,
    load_sem, a_send, a_recv, c_send, c_recv, p_send, p_recv, s_send, s_recv, g_send, g_recv,
):
    grp = lax.axis_index("grp")
    row = lax.axis_index("row")
    n_row = lax.axis_size("row")
    core = lax.rem(row, 2)
    half = lax.rem(grp, 2)

    def along_row(by):
        return (grp, lax.rem(row + by + n_row, n_row))

    def along_grp(by):
        return (lax.rem(grp + by, 4), row)

    partner = (jnp.where(core == 0, grp + 1 - 2 * half, 3 - grp), row)
    sibling = (grp, row + 1 - 2 * core)
    outside = along_row(2 * core - 1)

    def remote(src, dst, send, recv, device):
        return pltpu.make_async_remote_copy(
            src_ref=src, dst_ref=dst, send_sem=send, recv_sem=recv, device_id=device, device_id_type=MESH
        )

    load_p = pltpu.make_async_copy(p_hbm, p_own, load_sem.at[0])
    load_p_cols = pltpu.make_async_copy(p_cols_hbm, p_cols_v.at[:, pl.ds(128, 1024)], load_sem.at[1])
    load_c_cols = pltpu.make_async_copy(c_cols_hbm, c_cols_v.at[:, pl.ds(128, 512)], load_sem.at[2])
    load_a = pltpu.make_async_copy(a_hbm, a_own, load_sem.at[3])
    load_own_cols = pltpu.make_async_copy(a_cols_hbm, own_cols, load_sem.at[4])
    for load in (load_p, load_p_cols, load_c_cols, load_a, load_own_cols):
        load.start()

    barrier = pltpu.get_barrier_semaphore()
    peers = [along_grp(1), along_grp(2), along_grp(3)] + [along_row(by) for by in (1, -1, 2, -2)]
    for peer in peers:
        pl.semaphore_signal(barrier, inc=1, device_id=peer, device_id_type=MESH)

    lane = lax.broadcasted_iota(I32, (1, 128), 1)

    def from_lane(ref, start):
        begin = start + 128
        tile = begin // 128
        shift = lax.rem(begin, 128)
        first = pltpu.roll(ref[:, pl.ds(pl.multiple_of(tile * 128, 128), 128)], 128 - shift, 1)
        second = pltpu.roll(ref[:, pl.ds(pl.multiple_of(tile * 128 + 128, 128), 128)], 128 - shift, 1)
        return jnp.where(lane < 128 - shift, first, second)

    load_p_cols.wait()
    load_c_cols.wait()
    band_cols = from_lane(p_cols_v, row * 8 - 16)
    sub = lax.broadcasted_iota(I32, (32, 128), 0)
    place = jnp.full((32, 128), 4, I32)
    which = jnp.full((16, 128), 4, I32)
    for p in range(4):
        cols = band_cols[p : p + 1]
        place = jnp.where(cols - (row - 3) * 4 == sub, p, place)
        which = jnp.where(cols - (row - 1) * 4 == sub[:16], p, which)
    target = from_lane(c_cols_v, row * 4 - 4) - (row - 3) * 4
    tab_v[PLACE : PLACE + 32] = place
    tab_v[WHICH : WHICH + 16] = which
    tab_v[TARGET : TARGET + 16] = jnp.where((target >= 0) & (target < 28), target, 28)

    left = lax.broadcasted_iota(I32, (128, 128), 1) < 64

    def turn(x):
        return pltpu.roll(x.astype(F32), 64, 1).astype(x.dtype)

    load_p.wait()

    def halve(i, carry):
        for pair in range(2):
            x, y = p_own[i, 2 * pair], p_own[i, 2 * pair + 1]
            x_turned, y_turned = turn(x), turn(y)
            first = jnp.where(left, x, y_turned)
            second = jnp.where(left, x_turned, y)
            band[2, i, pair] = jnp.where(half == 0, first, second)
        return carry

    lax.fori_loop(0, 8, halve, 0)

    pl.semaphore_wait(barrier, len(peers))

    def a_copy(i):
        return remote(a_hbm.at[i], a_far.at[i], a_send.at[i], a_recv.at[i], partner)

    cols_copy = remote(a_cols_hbm, far_cols_v, c_send, c_recv, partner)
    cols_copy.start()
    for i in range(8):
        a_copy(i).start()

    sibling_slot = 3 - 2 * core
    there = 1 + 2 * core
    pass_slot = 4 - 4 * core
    other_slot = 4 * core
    passed_slot = 4 - sibling_slot

    def p_copy(kind, src, dst, n, device):
        lines = pl.ds(2 * n, 2)
        return remote(band.at[src, lines], band.at[dst, lines], p_send.at[kind, n], p_recv.at[dst, n], device)

    def p_next(n):
        return p_copy(0, 2, 0, n, along_row(2))

    def p_prev(n):
        return p_copy(1, 2, 4, n, along_row(-2))

    def p_sibling(n):
        return p_copy(2, 2, there, n, sibling)

    def p_pass(n):
        return p_copy(3, pass_slot, sibling_slot, n, sibling)

    for n in range(4):
        p_next(n).start()
        p_prev(n).start()
    for n in range(4):
        p_sibling(n).start()

    to_smem = pltpu.make_async_copy(tab_v, tab, load_sem.at[5])
    to_smem.start()

    def transpose(i, carry):
        for q in range(4):
            p_turn[i, q] = p_own[i, q].T
        p_turn[i, 4] = jnp.zeros((128, 128), BF16)
        window[i, 28] = jnp.zeros((128, 128), BF16)
        return carry

    lax.fori_loop(0, 8, transpose, 0)
    spreadable[4] = jnp.zeros((128, 128), BF16)
    to_smem.wait()

    def place_lines(slot, begin, count):
        def one(n, carry):
            line = slot * 8 + n
            for pair in range(2):
                x = band[slot, n, pair]
                turned = turn(x)
                spreadable[2 * pair] = jnp.where(left, x, turned)
                spreadable[2 * pair + 1] = jnp.where(left, turned, x)
            for w in range(14):
                first = spreadable[tab[PLACE + 2 * w, line]]
                second = spreadable[tab[PLACE + 2 * w + 1, line]]
                placed[line, w // 2, :, (w % 2) * 128 : (w % 2 + 1) * 128] = jnp.where(left, first, second)
            return carry

        lax.fori_loop(begin, begin + count, one, 0)

    def arrived(slot, n):
        p_copy(0, slot, slot, n, sibling).wait_recv()

    place_lines(2, 0, 8)
    for n in range(4):
        arrived(sibling_slot, n)
    place_lines(sibling_slot, 0, 8)

    def place_chunk(n, carry):
        arrived(pass_slot, n)
        p_pass(n).start()
        place_lines(pass_slot, 2 * n, 2)
        arrived(other_slot, n)
        place_lines(other_slot, 2 * n, 2)
        arrived(passed_slot, n)
        place_lines(passed_slot, 2 * n, 2)
        return carry

    lax.fori_loop(0, 4, place_chunk, 0)

    cols_copy.wait_recv()
    far_to_smem = pltpu.make_async_copy(far_cols_v, far_cols, load_sem.at[6])
    far_to_smem.start()
    load_own_cols.wait()
    load_a.wait()
    far_to_smem.wait()
    first_line = row * 8 - 16

    def fine_row(i, carry):
        a_copy(i).wait_recv()
        lhs = jnp.concatenate([a_own[i, s] for s in range(7)] + [a_far[i, s] for s in range(7)], axis=1)
        lines = [ref[s, 0, i] - first_line for ref in (own_cols, far_cols) for s in range(7)]
        lines = [jnp.clip(line, 0, 39) for line in lines]
        for n in range(7):
            rhs = jnp.concatenate([placed[line, n] for line in lines], axis=0)
            acc = jnp.dot(lhs, rhs, preferred_element_type=F32)
            for u in range(2):
                value = acc[:, u * 128 : (u + 1) * 128]
                high = value.astype(BF16).astype(F32)
                low = value - high
                window[i, 4 * n + 2 * u] = jnp.where(left, high, pltpu.roll(low, 64, 1)).astype(BF16)
                window[i, 4 * n + 2 * u + 1] = jnp.where(left, pltpu.roll(high, 64, 1), low).astype(BF16)
        return carry

    lax.fori_loop(0, 8, fine_row, 0)

    def unit(n):
        early = n < 12
        return jnp.where(early, n // 3, n - 12), jnp.where(early, lax.rem(n, 3), 3)

    def steps(t):
        return jnp.where(t == 0, 2, jnp.where(t == 1, 1, jnp.where(t == 2, 3, 0)))

    def coarse_tiles(c, t):
        lhs = jnp.concatenate([p_turn[i, tab[WHICH + c, 16 + i]] for i in range(8)], axis=1)
        k = TARGET + lax.rem(grp + steps(t), 4) * 4
        tiles = []
        for pair in range(2):
            first = tab[k + 2 * pair, c]
            second = tab[k + 2 * pair + 1, c]
            rhs = jnp.concatenate(
                [jnp.concatenate([window[i, first], window[i, second]], axis=1) for i in range(8)], axis=0
            )
            acc = jnp.dot(lhs, rhs, preferred_element_type=F32)
            x, y = acc[:, :128], acc[:, 128:]
            tiles.append(jnp.where(left, x, y) + pltpu.roll(jnp.where(left, y, x), 64, 1))
        return tiles

    def outer_copy(n):
        return remote(outer.at[n], from_outer.at[n], s_send.at[0, n], s_recv.at[0, n], outside)

    def inner_copy(n):
        return remote(inner.at[n], from_inner.at[n], s_send.at[1, n], s_recv.at[1, n], sibling)

    def group_copy(c, t):
        return remote(
            center.at[3 * c + t], gathered.at[t, c], g_send.at[t, c], g_recv.at[t, c], along_grp(steps(t))
        )

    def fill(ref, n, c, t):
        for pair, tile in enumerate(coarse_tiles(c, t)):
            ref[n, pair] = tile

    def absorb(n):
        outer_copy(n).wait_recv()
        inner_copy(n).wait_recv()
        center[n] = center[n] + (from_outer[n] + from_inner[n])

    def one_unit(n, carry):
        c, t = unit(n)

        @pl.when(n >= BEHIND)
        def _():
            absorb(n - BEHIND)

        fill(outer, n, c + 8 * core, t)

        @pl.when(n >= BEHIND)
        def _():
            done_c, done_t = unit(n - BEHIND)
            group_copy(done_c, done_t).start()

        fill(inner, n, c + 8 - 8 * core, t)
        outer_copy(n).start()
        fill(center, n, c + 4, t)
        inner_copy(n).start()
        return carry

    lax.fori_loop(0, 16, one_unit, 0)

    for c in range(4):
        absorb(12 + c)
        for t in range(3):
            group_copy(c, t).wait_recv()
        for pair in range(2):
            same = center[12 + c, pair] + gathered[0, c, pair]
            other = gathered[1, c, pair] + gathered[2, c, pair]
            x = jnp.where(half == 0, same, other)
            y = jnp.where(half == 0, other, same)
            out_v[c, 2 * pair] = jnp.where(left, x, pltpu.roll(y, 64, 1))
            out_v[c, 2 * pair + 1] = jnp.where(left, pltpu.roll(x, 64, 1), y)

    cols_copy.wait_send()
    for i in range(8):
        a_copy(i).wait_send()
    for n in range(4):
        for copy in (p_next(n), p_prev(n), p_sibling(n), p_pass(n)):
            copy.wait_send()

    def sent(n, carry):
        outer_copy(n).wait_send()
        inner_copy(n).wait_send()

        @pl.when(n < 12)
        def _():
            group_copy(n // 3, lax.rem(n, 3)).wait_send()

        return carry

    lax.fori_loop(0, 16, sent, 0)


def body(a_tiles, a_cols, p_tiles, p_cols, c_cols):
    dma = pltpu.SemaphoreType.DMA
    anywhere = pl.BlockSpec(memory_space=pl.ANY)
    side = pltpu.VMEM((16, 2, 128, 128), F32)
    return pl.pallas_call(
        kernel,
        out_shape=jax.ShapeDtypeStruct((4, 4, 128, 128), F32),
        in_specs=[anywhere] * 5,
        out_specs=pl.BlockSpec(memory_space=pltpu.VMEM),
        scratch_shapes=[
            pltpu.VMEM((8, 7, 128, 128), BF16),
            pltpu.VMEM((8, 7, 128, 128), BF16),
            pltpu.VMEM((8, 4, 128, 128), BF16),
            pltpu.VMEM((8, 5, 128, 128), BF16),
            pltpu.VMEM((5, 8, 2, 128, 128), BF16),
            pltpu.VMEM((5, 128, 128), BF16),
            pltpu.VMEM((40, 7, 128, 256), BF16),
            pltpu.VMEM((8, 29, 128, 128), BF16),
            side,
            side,
            side,
            side,
            side,
            pltpu.VMEM((3, 4, 2, 128, 128), F32),
            pltpu.VMEM((4, 1280), I32),
            pltpu.VMEM((16, 768), I32),
            pltpu.VMEM((7, 1, 8), I32),
            pltpu.VMEM((64, 128), I32),
            pltpu.SMEM((64, 128), I32),
            pltpu.SMEM((7, 1, 8), I32),
            pltpu.SMEM((7, 1, 8), I32),
            dma((7,)),
            dma((8,)),
            dma((8,)),
            dma,
            dma,
            dma((4, 4)),
            dma((5, 4)),
            dma((2, 16)),
            dma((2, 16)),
            dma((3, 4)),
            dma((3, 4)),
        ],
        compiler_params=pltpu.CompilerParams(
            collective_id=0, has_side_effects=True, vmem_limit_bytes=52 * 1024 * 1024
        ),
        cost_estimate=pl.CostEstimate(flops=4_000_000_000, bytes_accessed=8_000_000, transcendentals=0),
    )(
        a_cols.transpose(2, 1, 0), p_cols.T, c_cols.T, a_tiles.reshape(8, 7, 128, 128), p_tiles
    )


def solution(mesh):
    return jax.shard_map(
        body,
        mesh=mesh,
        in_specs=(
            P("row", "grp", None, None, None),
            P("row", "grp", None),
            P("row", None, None, None),
            P(),
            P(),
        ),
        out_specs=P("row", "grp", None, None),
        check_vma=False,
    )
```

time: 84.7 us -> 73.6 us (0.87)
  the two profiles are of different devices: /device:TPU:1 before, /device:TPU:8 now
where the time goes in v2:
time: 73.6 us; the launch traced here: 73.3 us
  Pallas kernels  70.2 us (95%)
  local copies, waits for them, and re-layouts  3.13 us (4%)
    pallas_call x1, Pallas kernels, body(): pl.pallas_call(kernel, out_shape=jax.ShapeDtypeStruct((4, 4, 128, 128), F...  70.2 us
    unnamed x7, local copies, waits for them, and re-layouts  3.13 us

profile of v2, /device:TPU:8, one launch (start us, length us, event | category | flops | bytes accessed | tf_op | source)
XLA Modules:
  0.0 73.3 jit_solution(6301903542696818030)
XLA Ops:
  0.0 0.0 copy-start
  0.0 0.8 %copy-done = s32[512,16]{0,1:T(8,128)S(1)} copy-done((s32[512,16]{0,1:T(8,128)S(1)}, s32[512,16]{0,1:T(8,128)}, u32[]{:S(2)}) %copy-start) | copy-done | bytes 32792
  0.8 0.0 copy-start.1
  0.8 0.7 copy-done.1
  1.5 0.0 copy-start.2
  1.5 0.7 copy-done.2
  2.2 70.2 %shard_map.55 = f32[4,4,128,128]{3,2,1,0:T(8,128)S(1)} custom-call(s32[7,1,8]{2,1,0:T(1,128)S(1)} %bitcast.6, s32[4,1024]{1,0:T(4,128)S(1)} %bitcast.5, s32[16,512]{1,0:T(8,128)S(1)} %bitcast.4, bf16[8,7,128,128]{3,2,1,0:T(8,128)(2,1)} %bitcast.7, bf16[8,4,128,128]{3,2,1,0:T(8,128)(2,1)} %p_hbm.1), custom_call_target="tpu_custom_call" | custom-call | flops 4000000000 | bytes 8000000 | tf_op jit(solution)/shard_map/pallas_call | solution.py:313
  72.3 1.0 %copy.7 = f32[4,4,128,128]{3,2,1,0:T(8,128)} copy(f32[4,4,128,128]{3,2,1,0:T(8,128)S(1)} %shard_map.55) | data formatting | bytes 2097152
Async XLA Ops:
  0.0 0.8 %copy-start = (s32[512,16]{0,1:T(8,128)S(1)}, s32[512,16]{0,1:T(8,128)}, u32[]{:S(2)}) copy-start(s32[512,16]{0,1:T(8,128)} %param.9) | copy-start | bytes 98308
  0.8 0.7 copy-start.1
  1.5 0.7 copy-start.2

commit v3 on v2

--- a/solution.py
+++ b/solution.py
@@ -9,15 +9,16 @@
 F32 = jnp.float32
 BF16 = jnp.bfloat16
 I32 = jnp.int32
-PLACE, WHICH, TARGET = 0, 32, 48
+PLACE, WHICH, TARGET, PAIR, COLUMN = 0, 32, 48, 64, 80
 BEHIND = 4
+BEHIND_FIRST = 8
 
 
 def kernel(
     a_cols_hbm, p_cols_hbm, c_cols_hbm, a_hbm, p_hbm, out_v,
     a_own, a_far, p_own, p_turn, band, spreadable, placed, window, outer, inner,
     from_outer, from_inner, center, gathered, p_cols_v, c_cols_v, far_cols_v, tab_v, tab, own_cols, far_cols,
-    load_sem, a_send, a_recv, c_send, c_recv, p_send, p_recv, s_send, s_recv, g_send, g_recv,
+    load_sem, a_send, a_recv, c_send, c_recv, p_send, p_recv, s_send, s_recv, g_send, g_recv, gate,
 ):
     grp = lax.axis_index("grp")
     row = lax.axis_index("row")
@@ -48,10 +49,38 @@
     for load in (load_p, load_p_cols, load_c_cols, load_a, load_own_cols):
         load.start()
 
+    place_z = lax.rem(row // 2, 16)
+    below = row >= 2
+    above = row < n_row - 2
+    first = (place_z == 0) & below
+    last = (place_z == 15) & above
+    has_outer = jnp.where(core == 0, row, n_row - 1 - row) >= 2
+
     barrier = pltpu.get_barrier_semaphore()
-    peers = [along_grp(1), along_grp(2), along_grp(3)] + [along_row(by) for by in (1, -1, 2, -2)]
-    for peer in peers:
-        pl.semaphore_signal(barrier, inc=1, device_id=peer, device_id_type=MESH)
+
+    def signal(semaphore, peer):
+        pl.semaphore_signal(semaphore, inc=1, device_id=peer, device_id_type=MESH)
+
+    for by in (1, 2, 3):
+        signal(barrier, along_grp(by))
+    signal(barrier, sibling)
+
+    @pl.when(below)
+    def _():
+        signal(barrier, along_row(-2))
+
+    @pl.when(below & (core == 0))
+    def _():
+        signal(barrier, along_row(-1))
+
+    @pl.when(above & jnp.logical_not(last))
+    def _():
+        signal(barrier, along_row(2))
+
+    @pl.when(above & jnp.logical_not(last) & (core == 1))
+    def _():
+        signal(barrier, along_row(1))
+
 
     lane = lax.broadcasted_iota(I32, (1, 128), 1)
 
@@ -69,16 +98,23 @@
     sub = lax.broadcasted_iota(I32, (32, 128), 0)
     place = jnp.full((32, 128), 4, I32)
     which = jnp.full((16, 128), 4, I32)
+    pair = jnp.full((16, 128), 160, I32)
     for p in range(4):
         cols = band_cols[p : p + 1]
-        place = jnp.where(cols - (row - 3) * 4 == sub, p, place)
+        column = cols - (row - 3) * 4
+        place = jnp.where(column == sub, p, place)
         which = jnp.where(cols - (row - 1) * 4 == sub[:16], p, which)
+        pair = jnp.where((column == 2 * sub[:16]) | (column == 2 * sub[:16] + 1), 4 * lane + p, pair)
+    columns = jnp.clip(band_cols - (row - 3) * 4, 0, 27)
     target = from_lane(c_cols_v, row * 4 - 4) - (row - 3) * 4
     tab_v[PLACE : PLACE + 32] = place
+    tab_v[PAIR : PAIR + 16] = pair
+    tab_v[COLUMN : COLUMN + 4] = columns - (columns & 1)
     tab_v[WHICH : WHICH + 16] = which
     tab_v[TARGET : TARGET + 16] = jnp.where((target >= 0) & (target < 28), target, 28)
 
     left = lax.broadcasted_iota(I32, (128, 128), 1) < 64
+    left16 = lax.broadcasted_iota(jnp.int16, (128, 128), 1) < 64
 
     def turn(x):
         return pltpu.roll(x.astype(F32), 64, 1).astype(x.dtype)
@@ -89,14 +125,21 @@
         for pair in range(2):
             x, y = p_own[i, 2 * pair], p_own[i, 2 * pair + 1]
             x_turned, y_turned = turn(x), turn(y)
-            first = jnp.where(left, x, y_turned)
-            second = jnp.where(left, x_turned, y)
-            band[2, i, pair] = jnp.where(half == 0, first, second)
+            band[2, i, pair] = jnp.where(half == 0, jnp.where(left, x, y_turned), jnp.where(left, x_turned, y))
         return carry
 
     lax.fori_loop(0, 8, halve, 0)
 
-    pl.semaphore_wait(barrier, len(peers))
+    pl.semaphore_wait(barrier, 4 + jnp.where(above, 1 + core, 0) + jnp.where(below & jnp.logical_not(first), 2 - core, 0))
+
+    @pl.when(last & (core == 1))
+    def _():
+        signal(gate, along_row(1))
+
+    @pl.when(last)
+    def _():
+        signal(gate, along_row(2))
+
 
     def a_copy(i):
         return remote(a_hbm.at[i], a_far.at[i], a_send.at[i], a_recv.at[i], partner)
@@ -106,15 +149,10 @@
     for i in range(8):
         a_copy(i).start()
 
-    sibling_slot = 3 - 2 * core
-    there = 1 + 2 * core
-    pass_slot = 4 - 4 * core
-    other_slot = 4 * core
-    passed_slot = 4 - sibling_slot
+    near = 3 - 2 * core
 
     def p_copy(kind, src, dst, n, device):
-        lines = pl.ds(2 * n, 2)
-        return remote(band.at[src, lines], band.at[dst, lines], p_send.at[kind, n], p_recv.at[dst, n], device)
+        return remote(band.at[src, n], band.at[dst, n], p_send.at[kind, n], p_recv.at[dst, n], device)
 
     def p_next(n):
         return p_copy(0, 2, 0, n, along_row(2))
@@ -123,15 +161,21 @@
         return p_copy(1, 2, 4, n, along_row(-2))
 
     def p_sibling(n):
-        return p_copy(2, 2, there, n, sibling)
+        return p_copy(2, 2, 4 - near, n, sibling)
 
     def p_pass(n):
-        return p_copy(3, pass_slot, sibling_slot, n, sibling)
-
-    for n in range(4):
-        p_next(n).start()
-        p_prev(n).start()
-    for n in range(4):
+        return p_copy(3, 4 - 4 * core, near, n, sibling)
+
+    for n in range(8):
+        @pl.when(above)
+        def _():
+            p_next(n).start()
+
+        @pl.when(below & jnp.logical_not(first))
+        def _():
+            p_prev(n).start()
+
+    for n in range(8):
         p_sibling(n).start()
 
     to_smem = pltpu.make_async_copy(tab_v, tab, load_sem.at[5])
@@ -146,6 +190,7 @@
 
     lax.fori_loop(0, 8, transpose, 0)
     spreadable[4] = jnp.zeros((128, 128), BF16)
+    placed[160] = jnp.zeros((128, 128), BF16)
     to_smem.wait()
 
     def place_lines(slot, begin, count):
@@ -154,12 +199,13 @@
             for pair in range(2):
                 x = band[slot, n, pair]
                 turned = turn(x)
-                spreadable[2 * pair] = jnp.where(left, x, turned)
-                spreadable[2 * pair + 1] = jnp.where(left, turned, x)
-            for w in range(14):
-                first = spreadable[tab[PLACE + 2 * w, line]]
-                second = spreadable[tab[PLACE + 2 * w + 1, line]]
-                placed[line, w // 2, :, (w % 2) * 128 : (w % 2 + 1) * 128] = jnp.where(left, first, second)
+                spreadable[2 * pair] = jnp.where(left16, x, turned)
+                spreadable[2 * pair + 1] = jnp.where(left16, turned, x)
+            for p in range(4):
+                column = tab[COLUMN + p, line]
+                before = spreadable[tab[PLACE + column, line]]
+                after = spreadable[tab[PLACE + 1 + column, line]]
+                placed[4 * line + p] = jnp.where(left16, before, after)
             return carry
 
         lax.fori_loop(begin, begin + count, one, 0)
@@ -167,22 +213,30 @@
     def arrived(slot, n):
         p_copy(0, slot, slot, n, sibling).wait_recv()
 
+    def there(slot):
+        return jnp.where(slot > 2, above, below)
+
+    def take(slot, n):
+        @pl.when(there(slot))
+        def _():
+            arrived(slot, n)
+
+            @pl.when(slot == 4 - 4 * core)
+            def _():
+                p_pass(n).start()
+
+            place_lines(slot, n, 1)
+
+    def follow(slot, n):
+        @pl.when((n >= 0) & (slot == 4 - near) & there(slot))
+        def _():
+            arrived(slot, n)
+            place_lines(slot, n, 1)
+
     place_lines(2, 0, 8)
-    for n in range(4):
-        arrived(sibling_slot, n)
-    place_lines(sibling_slot, 0, 8)
-
-    def place_chunk(n, carry):
-        arrived(pass_slot, n)
-        p_pass(n).start()
-        place_lines(pass_slot, 2 * n, 2)
-        arrived(other_slot, n)
-        place_lines(other_slot, 2 * n, 2)
-        arrived(passed_slot, n)
-        place_lines(passed_slot, 2 * n, 2)
-        return carry
-
-    lax.fori_loop(0, 4, place_chunk, 0)
+    for n in range(8):
+        arrived(near, n)
+    place_lines(near, 0, 8)
 
     cols_copy.wait_recv()
     far_to_smem = pltpu.make_async_copy(far_cols_v, far_cols, load_sem.at[6])
@@ -192,13 +246,18 @@
     far_to_smem.wait()
     first_line = row * 8 - 16
 
-    def fine_row(i, carry):
-        a_copy(i).wait_recv()
+    def fine_row(i, tiles):
         lhs = jnp.concatenate([a_own[i, s] for s in range(7)] + [a_far[i, s] for s in range(7)], axis=1)
         lines = [ref[s, 0, i] - first_line for ref in (own_cols, far_cols) for s in range(7)]
         lines = [jnp.clip(line, 0, 39) for line in lines]
-        for n in range(7):
-            rhs = jnp.concatenate([placed[line, n] for line in lines], axis=0)
+        for n in tiles:
+            rhs = jnp.concatenate(
+                [
+                    jnp.concatenate([placed[tab[PAIR + 2 * n + u, line]] for line in lines], axis=0)
+                    for u in range(2)
+                ],
+                axis=1,
+            )
             acc = jnp.dot(lhs, rhs, preferred_element_type=F32)
             for u in range(2):
                 value = acc[:, u * 128 : (u + 1) * 128]
@@ -206,9 +265,63 @@
                 low = value - high
                 window[i, 4 * n + 2 * u] = jnp.where(left, high, pltpu.roll(low, 64, 1)).astype(BF16)
                 window[i, 4 * n + 2 * u + 1] = jnp.where(left, pltpu.roll(high, 64, 1), low).astype(BF16)
-        return carry
-
-    lax.fori_loop(0, 8, fine_row, 0)
+
+    def whole_row(i, carry):
+        a_copy(i).wait_recv()
+        fine_row(i, range(7))
+        return carry
+
+    def two_rows(i, carry):
+        a_copy(2 * i).wait_recv()
+        a_copy(2 * i + 1).wait_recv()
+        fine_row(2 * i, range(7))
+        fine_row(2 * i + 1, range(7))
+        return carry
+
+    @pl.when(jnp.logical_not(first))
+    def _():
+        def take_both(n, carry):
+            take(4 - 4 * core, n)
+            take(4 * core, n)
+            follow(4 - near, n - 2)
+            return carry
+
+        lax.fori_loop(0, 8, take_both, 0)
+        follow(4 - near, 6)
+        follow(4 - near, 7)
+        lax.fori_loop(0, 3, two_rows, 0)
+        lax.fori_loop(6, 8, whole_row, 0)
+
+    @pl.when(first)
+    def _():
+        def take_upper(n, carry):
+            take(4, n)
+            follow(3, n - 2)
+            return carry
+
+        def upper_row(i, carry):
+            a_copy(i).wait_recv()
+            fine_row(i, range(4, 7))
+            take(0, i)
+            follow(1, i - 2)
+            return carry
+
+        def lower_rows(i, carry):
+            fine_row(2 * i, range(4))
+            fine_row(2 * i + 1, range(4))
+            return carry
+
+        lax.fori_loop(0, 4, take_upper, 0)
+        pl.semaphore_wait(gate, 2 - core)
+        for n in range(8):
+            p_prev(n).start()
+        lax.fori_loop(4, 8, take_upper, 0)
+        follow(3, 6)
+        follow(3, 7)
+        lax.fori_loop(0, 8, upper_row, 0)
+        follow(1, 6)
+        follow(1, 7)
+        lax.fori_loop(0, 4, lower_rows, 0)
 
     def unit(n):
         early = n < 12
@@ -248,34 +361,58 @@
             ref[n, pair] = tile
 
     def absorb(n):
-        outer_copy(n).wait_recv()
         inner_copy(n).wait_recv()
-        center[n] = center[n] + (from_outer[n] + from_inner[n])
+
+        @pl.when(has_outer)
+        def _():
+            outer_copy(n).wait_recv()
+            center[n] = center[n] + (from_outer[n] + from_inner[n])
+
+        @pl.when(jnp.logical_not(has_outer))
+        def _():
+            center[n] = center[n] + from_inner[n]
+
+    behind = jnp.where(first & (core == 0), BEHIND_FIRST, BEHIND)
 
     def one_unit(n, carry):
         c, t = unit(n)
 
-        @pl.when(n >= BEHIND)
-        def _():
-            absorb(n - BEHIND)
+        @pl.when(n >= behind)
+        def _():
+            absorb(n - behind)
 
         fill(outer, n, c + 8 * core, t)
 
-        @pl.when(n >= BEHIND)
-        def _():
-            done_c, done_t = unit(n - BEHIND)
+        @pl.when(n >= behind)
+        def _():
+            done_c, done_t = unit(n - behind)
             group_copy(done_c, done_t).start()
 
         fill(inner, n, c + 8 - 8 * core, t)
-        outer_copy(n).start()
+
+        @pl.when(has_outer)
+        def _():
+            outer_copy(n).start()
+
         fill(center, n, c + 4, t)
         inner_copy(n).start()
         return carry
 
     lax.fori_loop(0, 16, one_unit, 0)
 
+    def absorb_rest(n, carry):
+        absorb(n)
+
+        @pl.when((n > 16 - behind) & (n < 13))
+        def _():
+            done_c, done_t = unit(n - 1)
+            group_copy(done_c, done_t).start()
+
+        return carry
+
+    lax.fori_loop(16 - behind, 16, absorb_rest, 0)
+
     for c in range(4):
-        absorb(12 + c)
         for t in range(3):
             group_copy(c, t).wait_recv()
         for pair in range(2):
@@ -289,14 +426,28 @@
     cols_copy.wait_send()
     for i in range(8):
         a_copy(i).wait_send()
-    for n in range(4):
-        for copy in (p_next(n), p_prev(n), p_sibling(n), p_pass(n)):
-            copy.wait_send()
+    for n in range(8):
+        p_sibling(n).wait_send()
+
+        @pl.when(above)
+        def _():
+            p_next(n).wait_send()
+
+        @pl.when(below)
+        def _():
+            p_prev(n).wait_send()
+
+        @pl.when(there(4 - 4 * core))
+        def _():
+            p_pass(n).wait_send()
 
     def sent(n, carry):
-        outer_copy(n).wait_send()
         inner_copy(n).wait_send()
 
+        @pl.when(has_outer)
+        def _():
+            outer_copy(n).wait_send()
+
         @pl.when(n < 12)
         def _():
             group_copy(n // 3, lax.rem(n, 3)).wait_send()
@@ -307,12 +458,13 @@
 
 
 def body(a_tiles, a_cols, p_tiles, p_cols, c_cols):
+    operands = (a_cols.transpose(2, 1, 0), p_cols.T, c_cols.T, a_tiles.reshape(8, 7, 128, 128), p_tiles)
     dma = pltpu.SemaphoreType.DMA
     anywhere = pl.BlockSpec(memory_space=pl.ANY)
     side = pltpu.VMEM((16, 2, 128, 128), F32)
     return pl.pallas_call(
         kernel,
-        out_shape=jax.ShapeDtypeStruct((4, 4, 128, 128), F32),
+        out_shape=pltpu.VMEM((4, 4, 128, 128), F32),
         in_specs=[anywhere] * 5,
         out_specs=pl.BlockSpec(memory_space=pltpu.VMEM),
         scratch_shapes=[
@@ -322,7 +474,7 @@
             pltpu.VMEM((8, 5, 128, 128), BF16),
             pltpu.VMEM((5, 8, 2, 128, 128), BF16),
             pltpu.VMEM((5, 128, 128), BF16),
-            pltpu.VMEM((40, 7, 128, 256), BF16),
+            pltpu.VMEM((161, 128, 128), BF16),
             pltpu.VMEM((8, 29, 128, 128), BF16),
             side,
             side,
@@ -333,8 +485,8 @@
             pltpu.VMEM((4, 1280), I32),
             pltpu.VMEM((16, 768), I32),
             pltpu.VMEM((7, 1, 8), I32),
-            pltpu.VMEM((64, 128), I32),
-            pltpu.SMEM((64, 128), I32),
+            pltpu.VMEM((88, 128), I32),
+            pltpu.SMEM((88, 128), I32),
             pltpu.SMEM((7, 1, 8), I32),
             pltpu.SMEM((7, 1, 8), I32),
             dma((7,)),
@@ -342,20 +494,19 @@
             dma((8,)),
             dma,
             dma,
-            dma((4, 4)),
-            dma((5, 4)),
+            dma((4, 8)),
+            dma((5, 8)),
             dma((2, 16)),
             dma((2, 16)),
             dma((3, 4)),
             dma((3, 4)),
+            pltpu.SemaphoreType.REGULAR,
         ],
         compiler_params=pltpu.CompilerParams(
             collective_id=0, has_side_effects=True, vmem_limit_bytes=52 * 1024 * 1024
         ),
         cost_estimate=pl.CostEstimate(flops=4_000_000_000, bytes_accessed=8_000_000, transcendentals=0),
-    )(
-        a_cols.transpose(2, 1, 0), p_cols.T, c_cols.T, a_tiles.reshape(8, 7, 128, 128), p_tiles
-    )
+    )(*[pltpu.with_memory_space_constraint(x, pltpu.HBM) for x in operands])
 
 
 def solution(mesh):

time: 73.6 us -> 66.8 us (0.908)
  the two profiles are of different devices: /device:TPU:8 before, /device:TPU:6 now
where the time goes in v3:
time: 66.8 us; the launch traced here: 66.6 us
  Pallas kernels  65.7 us (98%)
  local copies, waits for them, and re-layouts  0.97 us (1%)
    pallas_call x1, Pallas kernels, body(): pl.pallas_call(kernel, out_shape=pltpu.VMEM((4, 4, 128, 128), F32), in_sp...  65.7 us

profile of v3, /device:TPU:6, one launch (start us, length us, event | category | flops | bytes accessed | tf_op | source)
XLA Modules:
  0.0 66.6 jit_solution(9573414979121537277)
XLA Ops:
  0.0 65.7 %shard_map.55 = f32[4,4,128,128]{3,2,1,0:T(8,128)S(1)} custom-call(s32[7,1,8]{2,1,0:T(1,128)} %bitcast.7, s32[4,1024]{1,0:T(4,128)} %bitcast.6, s32[16,512]{1,0:T(8,128)} %bitcast.5, bf16[8,7,128,128]{3,2,1,0:T(8,128)(2,1)} %bitcast.4, bf16[8,4,128,128]{3,2,1,0:T(8,128)(2,1)} %p_hbm.1), custom_call_target="tpu_custom_call" | custom-call | flops 4000000000 | bytes 8000000 | tf_op jit(solution)/shard_map/pallas_call | solution.py:465
  65.7 1.0 %copy.7 = f32[4,4,128,128]{3,2,1,0:T(8,128)} copy(f32[4,4,128,128]{3,2,1,0:T(8,128)S(1)} %shard_map.55) | data formatting | bytes 2097152

commit v4 on v3

--- a/solution.py
+++ b/solution.py
@@ -278,7 +278,15 @@
         fine_row(2 * i + 1, range(7))
         return carry
 
-    @pl.when(jnp.logical_not(first))
+    def tiles_of_two(tiles):
+        def two(i, carry):
+            fine_row(2 * i, tiles)
+            fine_row(2 * i + 1, tiles)
+            return carry
+
+        return two
+
+    @pl.when(jnp.logical_not(first | last))
     def _():
         def take_both(n, carry):
             take(4 - 4 * core, n)
@@ -292,6 +300,36 @@
         lax.fori_loop(0, 3, two_rows, 0)
         lax.fori_loop(6, 8, whole_row, 0)
 
+    @pl.when(last)
+    def _():
+        def take_late(n, carry):
+            take(0, n)
+            follow(1, n - 2)
+
+            @pl.when(n >= 2)
+            def _():
+                take(4, n - 2)
+
+            follow(3, n - 4)
+            return carry
+
+        lax.fori_loop(0, 8, take_late, 0)
+        follow(1, 6)
+        follow(1, 7)
+        for i in range(4):
+            a_copy(i).wait_recv()
+
+        def early(i, carry):
+            take(4, 6 + i)
+            return tiles_of_two(range(3))(i, carry)
+
+        lax.fori_loop(0, 2, early, 0)
+        for n in range(4, 8):
+            follow(3, n)
+        lax.fori_loop(0, 2, tiles_of_two(range(3, 7)), 0)
+        lax.fori_loop(2, 3, two_rows, 0)
+        lax.fori_loop(6, 8, whole_row, 0)
+
     @pl.when(first)
     def _():
         def take_upper(n, carry):
@@ -304,11 +342,6 @@
             fine_row(i, range(4, 7))
             take(0, i)
             follow(1, i - 2)
-            return carry
-
-        def lower_rows(i, carry):
-            fine_row(2 * i, range(4))
-            fine_row(2 * i + 1, range(4))
             return carry
 
         lax.fori_loop(0, 4, take_upper, 0)
@@ -321,7 +354,7 @@
         lax.fori_loop(0, 8, upper_row, 0)
         follow(1, 6)
         follow(1, 7)
-        lax.fori_loop(0, 4, lower_rows, 0)
+        lax.fori_loop(0, 4, tiles_of_two(range(4)), 0)
 
     def unit(n):
         early = n < 12
@@ -388,12 +421,11 @@
             done_c, done_t = unit(n - behind)
             group_copy(done_c, done_t).start()
 
+        @pl.when(has_outer)
+        def _():
+            outer_copy(n).start()
+
         fill(inner, n, c + 8 - 8 * core, t)
-
-        @pl.when(has_outer)
-        def _():
-            outer_copy(n).start()
-
         fill(center, n, c + 4, t)
         inner_copy(n).start()
         return carry

time: 66.8 us -> 65.5 us (0.981)
  Pallas kernels: 65.7 us -> 64.4 us
    pallas_call x1, Pallas kernels: 65.7 us -> 64.4 us  [body(): pl.pallas_call(kernel, out_shape=pltpu.VMEM((4, 4, 128, 128), F32), in_sp...]
where the time goes in v4:
time: 65.5 us; the launch traced here: 65.3 us
  Pallas kernels  64.4 us (98%)
  local copies, waits for them, and re-layouts  0.97 us (1%)
    pallas_call x1, Pallas kernels, body(): pl.pallas_call(kernel, out_shape=pltpu.VMEM((4, 4, 128, 128), F32), in_sp...  64.4 us

profile of v4, /device:TPU:6, one launch (start us, length us, event | category | flops | bytes accessed | tf_op | source)
XLA Modules:
  0.0 65.3 jit_solution(13514664919808573255)
XLA Ops:
  0.0 64.4 %shard_map.55 = f32[4,4,128,128]{3,2,1,0:T(8,128)S(1)} custom-call(s32[7,1,8]{2,1,0:T(1,128)} %bitcast.7, s32[4,1024]{1,0:T(4,128)} %bitcast.6, s32[16,512]{1,0:T(8,128)} %bitcast.5, bf16[8,7,128,128]{3,2,1,0:T(8,128)(2,1)} %bitcast.4, bf16[8,4,128,128]{3,2,1,0:T(8,128)(2,1)} %p_hbm.1), custom_call_target="tpu_custom_call" | custom-call | flops 4000000000 | bytes 8000000 | tf_op jit(solution)/shard_map/pallas_call | solution.py:497
  64.4 1.0 %copy.7 = f32[4,4,128,128]{3,2,1,0:T(8,128)} copy(f32[4,4,128,128]{3,2,1,0:T(8,128)S(1)} %shard_map.55) | data formatting | bytes 2097152

commit v5 on v3

--- a/solution.py
+++ b/solution.py
@@ -16,9 +16,9 @@
 
 def kernel(
     a_cols_hbm, p_cols_hbm, c_cols_hbm, a_hbm, p_hbm, out_v,
-    a_own, a_far, p_own, p_turn, band, spreadable, placed, window, outer, inner,
-    from_outer, from_inner, center, gathered, p_cols_v, c_cols_v, far_cols_v, tab_v, tab, own_cols, far_cols,
-    load_sem, a_send, a_recv, c_send, c_recv, p_send, p_recv, s_send, s_recv, g_send, g_recv, gate,
+    a_own, a_far, p_own, p_turn, band, begun, spreadable, placed, window, outer, inner,
+    from_outer, from_inner, center, gathered, terms, terms_in, sums, sums_in, p_cols_v, c_cols_v, far_cols_v, tab_v, tab, own_cols, far_cols,
+    load_sem, a_send, a_recv, c_send, c_recv, p_send, p_recv, s_send, s_recv, g_send, g_recv, t_send, t_recv, gate,
 ):
     grp = lax.axis_index("grp")
     row = lax.axis_index("row")
@@ -144,10 +144,16 @@
     def a_copy(i):
         return remote(a_hbm.at[i], a_far.at[i], a_send.at[i], a_recv.at[i], partner)
 
+    def last_copy(part):
+        slots = pl.ds(5 * part, 5 - 3 * part)
+        return remote(a_hbm.at[7, slots], a_far.at[7, slots], a_send.at[7 + part], a_recv.at[7 + part], partner)
+
     cols_copy = remote(a_cols_hbm, far_cols_v, c_send, c_recv, partner)
     cols_copy.start()
-    for i in range(8):
+    for i in range(7):
         a_copy(i).start()
+    for part in range(2):
+        last_copy(part).start()
 
     near = 3 - 2 * core
 
@@ -166,17 +172,22 @@
     def p_pass(n):
         return p_copy(3, 4 - 4 * core, near, n, sibling)
 
-    for n in range(8):
-        @pl.when(above)
-        def _():
-            p_next(n).start()
-
-        @pl.when(below & jnp.logical_not(first))
-        def _():
-            p_prev(n).start()
-
-    for n in range(8):
-        p_sibling(n).start()
+    def start_all(copy):
+        def one(n, carry):
+            copy(n).start()
+            return carry
+
+        lax.fori_loop(0, 8, one, 0)
+
+    @pl.when(above & (core == 1))
+    def _():
+        start_all(p_next)
+
+    @pl.when(below & jnp.logical_not(first) & (core == 0))
+    def _():
+        start_all(p_prev)
+
+    start_all(p_sibling)
 
     to_smem = pltpu.make_async_copy(tab_v, tab, load_sem.at[5])
     to_smem.start()
@@ -246,11 +257,12 @@
     far_to_smem.wait()
     first_line = row * 8 - 16
 
-    def fine_row(i, tiles):
-        lhs = jnp.concatenate([a_own[i, s] for s in range(7)] + [a_far[i, s] for s in range(7)], axis=1)
-        lines = [ref[s, 0, i] - first_line for ref in (own_cols, far_cols) for s in range(7)]
+    def tile_maker(i, slots):
+        lhs = jnp.concatenate([(a_own if s < 7 else a_far)[i, s % 7] for s in slots], axis=1)
+        lines = [(own_cols if s < 7 else far_cols)[s % 7, 0, i] - first_line for s in slots]
         lines = [jnp.clip(line, 0, 39) for line in lines]
-        for n in tiles:
+
+        def tile(n):
             rhs = jnp.concatenate(
                 [
                     jnp.concatenate([placed[tab[PAIR + 2 * n + u, line]] for line in lines], axis=0)
@@ -258,70 +270,152 @@
                 ],
                 axis=1,
             )
-            acc = jnp.dot(lhs, rhs, preferred_element_type=F32)
-            for u in range(2):
-                value = acc[:, u * 128 : (u + 1) * 128]
-                high = value.astype(BF16).astype(F32)
-                low = value - high
-                window[i, 4 * n + 2 * u] = jnp.where(left, high, pltpu.roll(low, 64, 1)).astype(BF16)
-                window[i, 4 * n + 2 * u + 1] = jnp.where(left, pltpu.roll(high, 64, 1), low).astype(BF16)
-
-    def whole_row(i, carry):
-        a_copy(i).wait_recv()
-        fine_row(i, range(7))
+            return jnp.dot(lhs, rhs, preferred_element_type=F32)
+
+        return tile
+
+    def split(i, n, acc):
+        for u in range(2):
+            value = acc[:, u * 128 : (u + 1) * 128]
+            high = value.astype(BF16).astype(F32)
+            low = value - high
+            window[i, 4 * n + 2 * u] = jnp.where(left, high, pltpu.roll(low, 64, 1)).astype(BF16)
+            window[i, 4 * n + 2 * u + 1] = jnp.where(left, pltpu.roll(high, 64, 1), low).astype(BF16)
+
+    def fine_row(i, begin, count):
+        tile = tile_maker(i, range(14))
+        for n in [begin + k for k in range(count)]:
+            split(i, n, tile(n))
+
+    def last_row():
+        last_copy(0).wait_recv()
+        tile = tile_maker(7, range(12))
+        for n in range(7):
+            begun[n] = tile(n)
+        last_copy(1).wait_recv()
+        tile = tile_maker(7, range(12, 14))
+        for n in range(7):
+            split(7, n, begun[n] + tile(n))
+
+    ahead = first & (core == 0)
+    late_near = last & (core == 0)
+    late_follow = last & (core == 1)
+
+    def follow_all(n, carry):
+        follow(4 - near, n)
+
+        @pl.when((n == 3) & late_near)
+        def _():
+            start_all(p_next)
+
+        return carry
+
+    def take_near(n, carry):
+        take(4 - 4 * core, n)
+
+        @pl.when(jnp.logical_not(ahead | last))
+        def _():
+            follow(4 - near, n - 2)
+
+        @pl.when((n == 5) & above & (core == 0) & jnp.logical_not(last))
+        def _():
+            start_all(p_next)
+
+        @pl.when((n == 5) & below & (core == 1))
+        def _():
+            @pl.when(first)
+            def _():
+                pl.semaphore_wait(gate, 1)
+
+            start_all(p_prev)
+
+        return carry
+
+    def take_far(n, carry):
+        take(4 * core, n)
+        return carry
+
+    def four_tiles(i, carry):
+        a_copy(2 * i).wait_recv()
+        a_copy(2 * i + 1).wait_recv()
+        fine_row(2 * i, 3 - 3 * core, 4)
+        fine_row(2 * i + 1, 3 - 3 * core, 4)
+        return carry
+
+    def other_three_tiles(i, carry):
+        fine_row(2 * i, 4 * core, 3)
+        fine_row(2 * i + 1, 4 * core, 3)
+        return carry
+
+    def three_tiles(i, carry):
+        a_copy(2 * i).wait_recv()
+        a_copy(2 * i + 1).wait_recv()
+        fine_row(2 * i, 0, 3)
+        fine_row(2 * i + 1, 0, 3)
+        return carry
+
+    def other_four_tiles(i, carry):
+        fine_row(2 * i, 3, 4)
+        fine_row(2 * i + 1, 3, 4)
         return carry
 
     def two_rows(i, carry):
         a_copy(2 * i).wait_recv()
         a_copy(2 * i + 1).wait_recv()
-        fine_row(2 * i, range(7))
-        fine_row(2 * i + 1, range(7))
-        return carry
-
-    @pl.when(jnp.logical_not(first))
-    def _():
-        def take_both(n, carry):
-            take(4 - 4 * core, n)
-            take(4 * core, n)
-            follow(4 - near, n - 2)
-            return carry
-
-        lax.fori_loop(0, 8, take_both, 0)
+        fine_row(2 * i, 0, 7)
+        fine_row(2 * i + 1, 0, 7)
+        return carry
+
+    def whole_row(i, carry):
+        a_copy(i).wait_recv()
+        fine_row(i, 0, 7)
+        return carry
+
+    @pl.when(late_near)
+    def _():
+        lax.fori_loop(0, 8, follow_all, 0)
+
+    lax.fori_loop(0, 8, take_near, 0)
+
+    @pl.when(ahead)
+    def _():
+        pl.semaphore_wait(gate, 2)
+        start_all(p_prev)
+        lax.fori_loop(0, 8, follow_all, 0)
+
+    @pl.when(jnp.logical_not(ahead | last))
+    def _():
         follow(4 - near, 6)
         follow(4 - near, 7)
-        lax.fori_loop(0, 3, two_rows, 0)
-        lax.fori_loop(6, 8, whole_row, 0)
-
-    @pl.when(first)
-    def _():
-        def take_upper(n, carry):
-            take(4, n)
-            follow(3, n - 2)
-            return carry
-
-        def upper_row(i, carry):
-            a_copy(i).wait_recv()
-            fine_row(i, range(4, 7))
-            take(0, i)
-            follow(1, i - 2)
-            return carry
-
-        def lower_rows(i, carry):
-            fine_row(2 * i, range(4))
-            fine_row(2 * i + 1, range(4))
-            return carry
-
-        lax.fori_loop(0, 4, take_upper, 0)
-        pl.semaphore_wait(gate, 2 - core)
-        for n in range(8):
-            p_prev(n).start()
-        lax.fori_loop(4, 8, take_upper, 0)
-        follow(3, 6)
-        follow(3, 7)
-        lax.fori_loop(0, 8, upper_row, 0)
-        follow(1, 6)
-        follow(1, 7)
-        lax.fori_loop(0, 4, lower_rows, 0)
+
+    pairs = jnp.where(ahead, 3, 2)
+
+    @pl.when(late_follow)
+    def _():
+        lax.fori_loop(0, 2, three_tiles, 0)
+        lax.fori_loop(0, 8, follow_all, 0)
+        lax.fori_loop(0, 8, take_far, 0)
+        lax.fori_loop(0, 2, other_four_tiles, 0)
+
+    @pl.when(jnp.logical_not(late_follow))
+    def _():
+        lax.fori_loop(0, pairs, four_tiles, 0)
+        lax.fori_loop(0, 8, take_far, 0)
+        lax.fori_loop(0, pairs, other_three_tiles, 0)
+
+    lax.fori_loop(pairs, 3, two_rows, 0)
+
+    whole_row(6, 0)
+
+    @pl.when(jnp.logical_not(last))
+    def _():
+        last_row()
+
+    @pl.when(last)
+    def _():
+        last_copy(0).wait_recv()
+        last_copy(1).wait_recv()
+        fine_row(7, 0, 7)
 
     def unit(n):
         early = n < 12
@@ -348,6 +442,31 @@
     def outer_copy(n):
         return remote(outer.at[n], from_outer.at[n], s_send.at[0, n], s_recv.at[0, n], outside)
 
+    sums_first = last & (core == 1)
+    gets_sums = first & (core == 0)
+
+    def by_sums(n):
+        return unit(n)[0] == 3
+
+    def sends_outer(n):
+        return has_outer & jnp.logical_not(sums_first & by_sums(n))
+
+    def gets_outer(n):
+        return has_outer & jnp.logical_not(gets_sums & by_sums(n))
+
+    def term_copy(t):
+        return remote(terms.at[t], terms_in.at[t], t_send.at[t], t_recv.at[t], along_grp(steps(t)))
+
+    def sums_copy():
+        return remote(sums, sums_in, t_send.at[3], t_recv.at[3], outside)
+
+    def whole_tiles(own, from_two, from_one, from_three):
+        same = own + from_two
+        other = from_one + from_three
+        x = jnp.where(half == 0, same, other)
+        y = jnp.where(half == 0, other, same)
+        return jnp.where(left, x, pltpu.roll(y, 64, 1)), jnp.where(left, pltpu.roll(x, 64, 1), y)
+
     def inner_copy(n):
         return remote(inner.at[n], from_inner.at[n], s_send.at[1, n], s_recv.at[1, n], sibling)
 
@@ -363,16 +482,34 @@
     def absorb(n):
         inner_copy(n).wait_recv()
 
-        @pl.when(has_outer)
+        @pl.when(gets_outer(n))
         def _():
             outer_copy(n).wait_recv()
-            center[n] = center[n] + (from_outer[n] + from_inner[n])
-
-        @pl.when(jnp.logical_not(has_outer))
-        def _():
-            center[n] = center[n] + from_inner[n]
+
+        center[n] = center[n] + (from_inner[n] + jnp.where(gets_outer(n), from_outer[n], 0.0))
 
     behind = jnp.where(first & (core == 0), BEHIND_FIRST, BEHIND)
+
+    def sum_first(n):
+        @pl.when(n < 4)
+        def _():
+            fill(terms, n, 11, n)
+
+        @pl.when((n > 0) & (n < 4))
+        def _():
+            term_copy(n - 1).start()
+
+        @pl.when(n == 8)
+        def _():
+            for t in range(3):
+                term_copy(t).wait_recv()
+            for pair in range(2):
+                tiles = whole_tiles(terms[3, pair], terms_in[0, pair], terms_in[1, pair], terms_in[2, pair])
+                sums[2 * pair], sums[2 * pair + 1] = tiles
+
+        @pl.when(n == 9)
+        def _():
+            sums_copy().start()
 
     def one_unit(n, carry):
         c, t = unit(n)
@@ -388,73 +525,99 @@
             done_c, done_t = unit(n - behind)
             group_copy(done_c, done_t).start()
 
+        @pl.when(sends_outer(n))
+        def _():
+            outer_copy(n).start()
+
         fill(inner, n, c + 8 - 8 * core, t)
-
-        @pl.when(has_outer)
-        def _():
-            outer_copy(n).start()
-
         fill(center, n, c + 4, t)
         inner_copy(n).start()
+
+        @pl.when(sums_first)
+        def _():
+            sum_first(n)
+
         return carry
 
     lax.fori_loop(0, 16, one_unit, 0)
 
-    def absorb_rest(n, carry):
-        absorb(n)
-
-        @pl.when((n > 16 - behind) & (n < 13))
-        def _():
-            done_c, done_t = unit(n - 1)
-            group_copy(done_c, done_t).start()
-
-        return carry
-
-    lax.fori_loop(16 - behind, 16, absorb_rest, 0)
-
-    for c in range(4):
+    cols_copy.wait_send()
+    for i in range(7):
+        a_copy(i).wait_send()
+    for part in range(2):
+        last_copy(part).wait_send()
+    for n in range(8):
+        p_sibling(n).wait_send()
+
+        @pl.when(above)
+        def _():
+            p_next(n).wait_send()
+
+        @pl.when(below)
+        def _():
+            p_prev(n).wait_send()
+
+        @pl.when(there(4 - 4 * core))
+        def _():
+            p_pass(n).wait_send()
+
+    def finish(c):
         for t in range(3):
             group_copy(c, t).wait_recv()
         for pair in range(2):
-            same = center[12 + c, pair] + gathered[0, c, pair]
-            other = gathered[1, c, pair] + gathered[2, c, pair]
-            x = jnp.where(half == 0, same, other)
-            y = jnp.where(half == 0, other, same)
-            out_v[c, 2 * pair] = jnp.where(left, x, pltpu.roll(y, 64, 1))
-            out_v[c, 2 * pair + 1] = jnp.where(left, pltpu.roll(x, 64, 1), y)
-
-    cols_copy.wait_send()
-    for i in range(8):
-        a_copy(i).wait_send()
-    for n in range(8):
-        p_sibling(n).wait_send()
-
-        @pl.when(above)
-        def _():
-            p_next(n).wait_send()
-
-        @pl.when(below)
-        def _():
-            p_prev(n).wait_send()
-
-        @pl.when(there(4 - 4 * core))
-        def _():
-            p_pass(n).wait_send()
+            tiles = whole_tiles(
+                center[12 + c, pair], gathered[0, c, pair], gathered[1, c, pair], gathered[2, c, pair]
+            )
+            out_v[c, 2 * pair], out_v[c, 2 * pair + 1] = tiles
+
+    def absorb_rest(n, carry):
+        absorb(n)
+
+        @pl.when((n > 16 - behind) & (n < 13))
+        def _():
+            done_c, done_t = unit(n - 1)
+            group_copy(done_c, done_t).start()
+
+        @pl.when(n >= 13)
+        def _():
+            finish(n - 13)
+
+        return carry
+
+    lax.fori_loop(16 - behind, 15, absorb_rest, 0)
+    finish(2)
 
     def sent(n, carry):
         inner_copy(n).wait_send()
 
-        @pl.when(has_outer)
+        @pl.when(sends_outer(n))
         def _():
             outer_copy(n).wait_send()
 
-        @pl.when(n < 12)
+        @pl.when(n < 9)
         def _():
             group_copy(n // 3, lax.rem(n, 3)).wait_send()
 
         return carry
 
-    lax.fori_loop(0, 16, sent, 0)
+    lax.fori_loop(0, 15, sent, 0)
+    absorb(15)
+    finish(3)
+
+    @pl.when(gets_sums)
+    def _():
+        sums_copy().wait_recv()
+        out_v[3] = out_v[3] + sums_in[...]
+
+    @pl.when(sums_first)
+    def _():
+        for t in range(3):
+            term_copy(t).wait_send()
+        sums_copy().wait_send()
+
+    sent(15, 0)
+    for t in range(3):
+        group_copy(3, t).wait_send()
 
 
 def body(a_tiles, a_cols, p_tiles, p_cols, c_cols):
@@ -473,6 +636,7 @@
             pltpu.VMEM((8, 4, 128, 128), BF16),
             pltpu.VMEM((8, 5, 128, 128), BF16),
             pltpu.VMEM((5, 8, 2, 128, 128), BF16),
+            pltpu.VMEM((7, 128, 256), F32),
             pltpu.VMEM((5, 128, 128), BF16),
             pltpu.VMEM((161, 128, 128), BF16),
             pltpu.VMEM((8, 29, 128, 128), BF16),
@@ -482,6 +646,10 @@
             side,
             side,
             pltpu.VMEM((3, 4, 2, 128, 128), F32),
+            pltpu.VMEM((4, 2, 128, 128), F32),
+            pltpu.VMEM((3, 2, 128, 128), F32),
+            pltpu.VMEM((4, 128, 128), F32),
+            pltpu.VMEM((4, 128, 128), F32),
             pltpu.VMEM((4, 1280), I32),
             pltpu.VMEM((16, 768), I32),
             pltpu.VMEM((7, 1, 8), I32),
@@ -490,8 +658,8 @@
             pltpu.SMEM((7, 1, 8), I32),
             pltpu.SMEM((7, 1, 8), I32),
             dma((7,)),
-            dma((8,)),
-            dma((8,)),
+            dma((9,)),
+            dma((9,)),
             dma,
             dma,
             dma((4, 8)),
@@ -500,6 +668,8 @@
             dma((2, 16)),
             dma((3, 4)),
             dma((3, 4)),
+            dma((4,)),
+            dma((4,)),
             pltpu.SemaphoreType.REGULAR,
         ],
         compiler_params=pltpu.CompilerParams(

time: 66.8 us -> 64.3 us (0.963)
  Pallas kernels: 65.7 us -> 63 us
    pallas_call x1, Pallas kernels: 65.7 us -> 63 us  [body(): pl.pallas_call(kernel, out_shape=pltpu.VMEM((4, 4, 128, 128), F32), in_sp...]
where the time goes in v5:
time: 64.3 us; the launch traced here: 64 us
  Pallas kernels  63 us (98%)
  local copies, waits for them, and re-layouts  0.97 us (2%)
    pallas_call x1, Pallas kernels, body(): pl.pallas_call(kernel, out_shape=pltpu.VMEM((4, 4, 128, 128), F32), in_sp...  63 us

profile of v5, /device:TPU:6, one launch (start us, length us, event | category | flops | bytes accessed | tf_op | source)
XLA Modules:
  0.0 64.0 jit_solution(16857320890474632608)
XLA Ops:
  0.0 63.0 %shard_map.55 = f32[4,4,128,128]{3,2,1,0:T(8,128)S(1)} custom-call(s32[7,1,8]{2,1,0:T(1,128)} %bitcast.7, s32[4,1024]{1,0:T(4,128)} %bitcast.6, s32[16,512]{1,0:T(8,128)} %bitcast.5, bf16[8,7,128,128]{3,2,1,0:T(8,128)(2,1)} %bitcast.4, bf16[8,4,128,128]{3,2,1,0:T(8,128)(2,1)} %p_hbm.1), custom_call_target="tpu_custom_call" | custom-call | flops 4000000000 | bytes 8000000 | tf_op jit(solution)/shard_map/pallas_call | solution.py:628
  63.0 1.0 %copy.7 = f32[4,4,128,128]{3,2,1,0:T(8,128)} copy(f32[4,4,128,128]{3,2,1,0:T(8,128)S(1)} %shard_map.55) | data formatting | bytes 2097152

commit v6 on v5

--- a/solution.py
+++ b/solution.py
@@ -10,8 +10,8 @@
 BF16 = jnp.bfloat16
 I32 = jnp.int32
 PLACE, WHICH, TARGET, PAIR, COLUMN = 0, 32, 48, 64, 80
-BEHIND = 4
-BEHIND_FIRST = 8
+BEHIND = 3
+BEHIND_FIRST = 6
 
 
 def kernel(
@@ -300,6 +300,7 @@
     ahead = first & (core == 0)
     late_near = last & (core == 0)
     late_follow = last & (core == 1)
+    late_take = first & (core == 1)
 
     def follow_all(n, carry):
         follow(4 - near, n)
@@ -316,6 +317,10 @@
         @pl.when(jnp.logical_not(ahead | last))
         def _():
             follow(4 - near, n - 2)
+
+        @pl.when(late_take)
+        def _():
+            take(4 * core, n)
 
         @pl.when((n == 5) & above & (core == 0) & jnp.logical_not(last))
         def _():
@@ -400,7 +405,7 @@
     @pl.when(jnp.logical_not(late_follow))
     def _():
         lax.fori_loop(0, pairs, four_tiles, 0)
-        lax.fori_loop(0, 8, take_far, 0)
+        lax.fori_loop(jnp.where(late_take, 8, 0), 8, take_far, 0)
         lax.fori_loop(0, pairs, other_three_tiles, 0)
 
     lax.fori_loop(pairs, 3, two_rows, 0)
@@ -446,7 +451,7 @@
     gets_sums = first & (core == 0)
 
     def by_sums(n):
-        return unit(n)[0] == 3
+        return unit(n)[0] == 0
 
     def sends_outer(n):
         return has_outer & jnp.logical_not(sums_first & by_sums(n))
@@ -493,7 +498,7 @@
     def sum_first(n):
         @pl.when(n < 4)
         def _():
-            fill(terms, n, 11, n)
+            fill(terms, n, 8, n)
 
         @pl.when((n > 0) & (n < 4))
         def _():
@@ -514,24 +519,30 @@
     def one_unit(n, carry):
         c, t = unit(n)
 
-        @pl.when(n >= behind)
-        def _():
-            absorb(n - behind)
-
-        fill(outer, n, c + 8 * core, t)
-
-        @pl.when(n >= behind)
-        def _():
-            done_c, done_t = unit(n - behind)
+        soon = gets_sums & (n >= 2) & (n < 5)
+        done = jnp.where(soon, n - 2, n - behind)
+        taken = (n >= behind + jnp.where(gets_sums, 3, 0)) | soon
+
+        @pl.when(taken)
+        def _():
+            absorb(done)
+
+        m = jnp.where(sums_first, jnp.where(n < 9, n + 3, jnp.where(n < 12, n + 4, 0)), n)
+        outer_c, outer_t = unit(m)
+        fill(outer, m, outer_c + 8 * core, outer_t)
+
+        @pl.when(taken & (done < 12))
+        def _():
+            done_c, done_t = unit(done)
             group_copy(done_c, done_t).start()
 
-        @pl.when(sends_outer(n))
-        def _():
-            outer_copy(n).start()
+        @pl.when(has_outer & jnp.logical_not(sums_first & (n >= 12)))
+        def _():
+            outer_copy(m).start()
 
         fill(inner, n, c + 8 - 8 * core, t)
+        inner_copy(n).start()
         fill(center, n, c + 4, t)
-        inner_copy(n).start()
 
         @pl.when(sums_first)
         def _():
@@ -607,7 +618,7 @@
     @pl.when(gets_sums)
     def _():
         sums_copy().wait_recv()
-        out_v[3] = out_v[3] + sums_in[...]
+        out_v[0] = out_v[0] + sums_in[...]
 
     @pl.when(sums_first)
     def _():

time: 64.3 us -> 63.4 us (0.986)
  Pallas kernels: 63 us -> 62.3 us
    pallas_call x1, Pallas kernels: 63 us -> 62.3 us  [body(): pl.pallas_call(kernel, out_shape=pltpu.VMEM((4, 4, 128, 128), F32), in_sp...]
where the time goes in v6:
time: 63.4 us; the launch traced here: 63.3 us
  Pallas kernels  62.3 us (98%)
  local copies, waits for them, and re-layouts  0.97 us (2%)
    pallas_call x1, Pallas kernels, body(): pl.pallas_call(kernel, out_shape=pltpu.VMEM((4, 4, 128, 128), F32), in_sp...  62.3 us

profile of v6, /device:TPU:6, one launch (start us, length us, event | category | flops | bytes accessed | tf_op | source)
XLA Modules:
  0.0 63.3 jit_solution(16714282420966865070)
XLA Ops:
  0.0 62.3 %shard_map.55 = f32[4,4,128,128]{3,2,1,0:T(8,128)S(1)} custom-call(s32[7,1,8]{2,1,0:T(1,128)} %bitcast.7, s32[4,1024]{1,0:T(4,128)} %bitcast.6, s32[16,512]{1,0:T(8,128)} %bitcast.5, bf16[8,7,128,128]{3,2,1,0:T(8,128)(2,1)} %bitcast.4, bf16[8,4,128,128]{3,2,1,0:T(8,128)(2,1)} %p_hbm.1), custom_call_target="tpu_custom_call" | custom-call | flops 4000000000 | bytes 8000000 | tf_op jit(solution)/shard_map/pallas_call | solution.py:639
  62.3 1.0 %copy.7 = f32[4,4,128,128]{3,2,1,0:T(8,128)} copy(f32[4,4,128,128]{3,2,1,0:T(8,128)S(1)} %shard_map.55) | data formatting | bytes 2097152

commit v7 on v6

--- a/solution.py
+++ b/solution.py
@@ -11,7 +11,7 @@
 I32 = jnp.int32
 PLACE, WHICH, TARGET, PAIR, COLUMN = 0, 32, 48, 64, 80
 BEHIND = 3
-BEHIND_FIRST = 6
+BEHIND_FIRST = 7
 
 
 def kernel(
@@ -92,43 +92,50 @@
         second = pltpu.roll(ref[:, pl.ds(pl.multiple_of(tile * 128 + 128, 128), 128)], 128 - shift, 1)
         return jnp.where(lane < 128 - shift, first, second)
 
-    load_p_cols.wait()
-    load_c_cols.wait()
-    band_cols = from_lane(p_cols_v, row * 8 - 16)
-    sub = lax.broadcasted_iota(I32, (32, 128), 0)
-    place = jnp.full((32, 128), 4, I32)
-    which = jnp.full((16, 128), 4, I32)
-    pair = jnp.full((16, 128), 160, I32)
-    for p in range(4):
-        cols = band_cols[p : p + 1]
-        column = cols - (row - 3) * 4
-        place = jnp.where(column == sub, p, place)
-        which = jnp.where(cols - (row - 1) * 4 == sub[:16], p, which)
-        pair = jnp.where((column == 2 * sub[:16]) | (column == 2 * sub[:16] + 1), 4 * lane + p, pair)
-    columns = jnp.clip(band_cols - (row - 3) * 4, 0, 27)
-    target = from_lane(c_cols_v, row * 4 - 4) - (row - 3) * 4
-    tab_v[PLACE : PLACE + 32] = place
-    tab_v[PAIR : PAIR + 16] = pair
-    tab_v[COLUMN : COLUMN + 4] = columns - (columns & 1)
-    tab_v[WHICH : WHICH + 16] = which
-    tab_v[TARGET : TARGET + 16] = jnp.where((target >= 0) & (target < 28), target, 28)
-
     left = lax.broadcasted_iota(I32, (128, 128), 1) < 64
     left16 = lax.broadcasted_iota(jnp.int16, (128, 128), 1) < 64
 
     def turn(x):
         return pltpu.roll(x.astype(F32), 64, 1).astype(x.dtype)
 
-    load_p.wait()
-
-    def halve(i, carry):
-        for pair in range(2):
-            x, y = p_own[i, 2 * pair], p_own[i, 2 * pair + 1]
-            x_turned, y_turned = turn(x), turn(y)
-            band[2, i, pair] = jnp.where(half == 0, jnp.where(left, x, y_turned), jnp.where(left, x_turned, y))
-        return carry
-
-    lax.fori_loop(0, 8, halve, 0)
+    def prepare():
+        load_p_cols.wait()
+        load_c_cols.wait()
+        band_cols = from_lane(p_cols_v, row * 8 - 16)
+        sub = lax.broadcasted_iota(I32, (32, 128), 0)
+        place = jnp.full((32, 128), 4, I32)
+        which = jnp.full((16, 128), 4, I32)
+        pair = jnp.full((16, 128), 160, I32)
+        for p in range(4):
+            cols = band_cols[p : p + 1]
+            column = cols - (row - 3) * 4
+            place = jnp.where(column == sub, p, place)
+            which = jnp.where(cols - (row - 1) * 4 == sub[:16], p, which)
+            pair = jnp.where((column == 2 * sub[:16]) | (column == 2 * sub[:16] + 1), 4 * lane + p, pair)
+        columns = jnp.clip(band_cols - (row - 3) * 4, 0, 27)
+        target = from_lane(c_cols_v, row * 4 - 4) - (row - 3) * 4
+        tab_v[PLACE : PLACE + 32] = place
+        tab_v[PAIR : PAIR + 16] = pair
+        tab_v[COLUMN : COLUMN + 4] = columns - (columns & 1)
+        tab_v[WHICH : WHICH + 16] = which
+        tab_v[TARGET : TARGET + 16] = jnp.where((target >= 0) & (target < 28), target, 28)
+
+        load_p.wait()
+
+        def halve(i, carry):
+            for pair in range(2):
+                x, y = p_own[i, 2 * pair], p_own[i, 2 * pair + 1]
+                x_turned, y_turned = turn(x), turn(y)
+                band[2, i, pair] = jnp.where(half == 0, jnp.where(left, x, y_turned), jnp.where(left, x_turned, y))
+            return carry
+
+        lax.fori_loop(0, 8, halve, 0)
+
+    early = (grp < 2) | (place_z < 8)
+
+    @pl.when(early)
+    def _():
+        prepare()
 
     pl.semaphore_wait(barrier, 4 + jnp.where(above, 1 + core, 0) + jnp.where(below & jnp.logical_not(first), 2 - core, 0))
 
@@ -154,6 +161,10 @@
         a_copy(i).start()
     for part in range(2):
         last_copy(part).start()
+
+    @pl.when(jnp.logical_not(early))
+    def _():
+        prepare()
 
     near = 3 - 2 * core
 
@@ -305,7 +316,7 @@
     def follow_all(n, carry):
         follow(4 - near, n)
 
-        @pl.when((n == 3) & late_near)
+        @pl.when((n == 1) & late_near)
         def _():
             start_all(p_next)
 
@@ -326,7 +337,7 @@
         def _():
             start_all(p_next)
 
-        @pl.when((n == 5) & below & (core == 1))
+        @pl.when((n == jnp.where(first, 3, 5)) & below & (core == 1))
         def _():
             @pl.when(first)
             def _():
@@ -612,13 +623,13 @@
         return carry
 
     lax.fori_loop(0, 15, sent, 0)
+    @pl.when(gets_sums)
+    def _():
+        sums_copy().wait_recv()
+        out_v[0] = out_v[0] + sums_in[...]
+
     absorb(15)
     finish(3)
-
-    @pl.when(gets_sums)
-    def _():
-        sums_copy().wait_recv()
-        out_v[0] = out_v[0] + sums_in[...]
 
     @pl.when(sums_first)
     def _():

time: 63.4 us -> 62.9 us (level)
  no operation moved by 1% of the time
where the time goes in v7:
time: 62.9 us; the launch traced here: 62.8 us
  Pallas kernels  61.8 us (98%)
  local copies, waits for them, and re-layouts  0.97 us (2%)
    pallas_call x1, Pallas kernels, body(): pl.pallas_call(kernel, out_shape=pltpu.VMEM((4, 4, 128, 128), F32), in_sp...  61.8 us

profile of v7, /device:TPU:6, one launch (start us, length us, event | category | flops | bytes accessed | tf_op | source)
XLA Modules:
  0.0 62.8 jit_solution(5202540924307844790)
XLA Ops:
  0.0 61.8 %shard_map.55 = f32[4,4,128,128]{3,2,1,0:T(8,128)S(1)} custom-call(s32[7,1,8]{2,1,0:T(1,128)} %bitcast.7, s32[4,1024]{1,0:T(4,128)} %bitcast.6, s32[16,512]{1,0:T(8,128)} %bitcast.5, bf16[8,7,128,128]{3,2,1,0:T(8,128)(2,1)} %bitcast.4, bf16[8,4,128,128]{3,2,1,0:T(8,128)(2,1)} %p_hbm.1), custom_call_target="tpu_custom_call" | custom-call | flops 4000000000 | bytes 8000000 | tf_op jit(solution)/shard_map/pallas_call | solution.py:650
  61.8 1.0 %copy.7 = f32[4,4,128,128]{3,2,1,0:T(8,128)} copy(f32[4,4,128,128]{3,2,1,0:T(8,128)S(1)} %shard_map.55) | data formatting | bytes 2097152

commit v8 on v7

--- a/solution.py
+++ b/solution.py
@@ -504,7 +504,7 @@
 
         center[n] = center[n] + (from_inner[n] + jnp.where(gets_outer(n), from_outer[n], 0.0))
 
-    behind = jnp.where(first & (core == 0), BEHIND_FIRST, BEHIND)
+    behind = jnp.where(first & (core == 0), BEHIND_FIRST, jnp.where(last & (core == 1), BEHIND + 2, BEHIND))
 
     def sum_first(n):
         @pl.when(n < 4)
@@ -523,7 +523,7 @@
                 tiles = whole_tiles(terms[3, pair], terms_in[0, pair], terms_in[1, pair], terms_in[2, pair])
                 sums[2 * pair], sums[2 * pair + 1] = tiles
 
-        @pl.when(n == 9)
+        @pl.when(n == 12)
         def _():
             sums_copy().start()
 

time: 62.9 us -> 62.9 us (level)
  no operation moved by 1% of the time
where the time goes in v8:
time: 62.9 us; the launch traced here: 62.8 us
  Pallas kernels  61.8 us (98%)
  local copies, waits for them, and re-layouts  0.97 us (2%)
    pallas_call x1, Pallas kernels, body(): pl.pallas_call(kernel, out_shape=pltpu.VMEM((4, 4, 128, 128), F32), in_sp...  61.8 us

profile of v8, /device:TPU:6, one launch (start us, length us, event | category | flops | bytes accessed | tf_op | source)
XLA Modules:
  0.0 62.8 jit_solution(15673207579833138677)
XLA Ops:
  0.0 61.8 %shard_map.55 = f32[4,4,128,128]{3,2,1,0:T(8,128)S(1)} custom-call(s32[7,1,8]{2,1,0:T(1,128)} %bitcast.7, s32[4,1024]{1,0:T(4,128)} %bitcast.6, s32[16,512]{1,0:T(8,128)} %bitcast.5, bf16[8,7,128,128]{3,2,1,0:T(8,128)(2,1)} %bitcast.4, bf16[8,4,128,128]{3,2,1,0:T(8,128)(2,1)} %p_hbm.1), custom_call_target="tpu_custom_call" | custom-call | flops 4000000000 | bytes 8000000 | tf_op jit(solution)/shard_map/pallas_call | solution.py:650
  61.8 1.0 %copy.7 = f32[4,4,128,128]{3,2,1,0:T(8,128)} copy(f32[4,4,128,128]{3,2,1,0:T(8,128)S(1)} %shard_map.55) | data formatting | bytes 2097152

commit v9 on v8

--- a/solution.py
+++ b/solution.py
@@ -504,7 +504,7 @@
 
         center[n] = center[n] + (from_inner[n] + jnp.where(gets_outer(n), from_outer[n], 0.0))
 
-    behind = jnp.where(first & (core == 0), BEHIND_FIRST, jnp.where(last & (core == 1), BEHIND + 2, BEHIND))
+    behind = jnp.where(first & (core == 0), BEHIND_FIRST, BEHIND)
 
     def sum_first(n):
         @pl.when(n < 4)

time: 62.9 us -> 62.9 us (level)
  no operation moved by 1% of the time
where the time goes in v9:
time: 62.9 us; the launch traced here: 62.8 us
  Pallas kernels  61.8 us (98%)
  local copies, waits for them, and re-layouts  0.97 us (2%)
    pallas_call x1, Pallas kernels, body(): pl.pallas_call(kernel, out_shape=pltpu.VMEM((4, 4, 128, 128), F32), in_sp...  61.8 us

profile of v9, /device:TPU:6, one launch (start us, length us, event | category | flops | bytes accessed | tf_op | source)
XLA Modules:
  0.0 62.8 jit_solution(7082678033784443083)
XLA Ops:
  0.0 61.8 %shard_map.55 = f32[4,4,128,128]{3,2,1,0:T(8,128)S(1)} custom-call(s32[7,1,8]{2,1,0:T(1,128)} %bitcast.7, s32[4,1024]{1,0:T(4,128)} %bitcast.6, s32[16,512]{1,0:T(8,128)} %bitcast.5, bf16[8,7,128,128]{3,2,1,0:T(8,128)(2,1)} %bitcast.4, bf16[8,4,128,128]{3,2,1,0:T(8,128)(2,1)} %p_hbm.1), custom_call_target="tpu_custom_call" | custom-call | flops 4000000000 | bytes 8000000 | tf_op jit(solution)/shard_map/pallas_call | solution.py:650
  61.8 1.0 %copy.7 = f32[4,4,128,128]{3,2,1,0:T(8,128)} copy(f32[4,4,128,128]{3,2,1,0:T(8,128)S(1)} %shard_map.55) | data formatting | bytes 2097152
